TPU v7x, 32 devices: a whole 2x2x4 slice. The times are simulated.
32 devices in a mesh: dp: 4 (over y, core), seq: 8 (over z, x).
Axes of the slice: x: 2, y: 2, z: 4, core: 2. Of those that a mesh axis runs over, the one named last changes fastest.
Arguments:
- head_inputs: bfloat16 [4, 3072, 1024], P('dp', 'seq'), may hold values from -6 to 6
- gate_inputs: bfloat16 [4, 3072, 1024], P('dp', 'seq'), may hold values from -6 to 6
- state_proj: bfloat16 [4, 3072, 256], P('dp', 'seq'), may hold values from -2 to 2
- time_steps: float32 [4, 3072, 16], P('dp', 'seq'), may hold values from -4.7 to 4.7
- token_ids: int32 [4, 3072], P('dp', 'seq'), may hold values from 0 to 50279, as said below
- token_counts: int32 [4], replicated, may hold values from 1536 to 3072
- teacher_out: bfloat16 [4, 3072, 1024], P('dp', 'seq'), may hold values from -6 to 6
- out_weight: float32 [1024, 1024], P(('dp', 'seq')), may hold values from -0.1875 to 0.1875
- decay_log: float32 [16], replicated, may hold values from -6.5 to 1
- step_bias: float32 [16], replicated, may hold values from -5 to -3
- skip_gain: float32 [16], replicated, may hold values from 0.5 to 1.5
- norm_gain: float32 [1024], replicated, may hold values from 0.5 to 1.5
Outputs:
- losses: float32 [2], replicated
- new_weight: float32 [1024, 1024], P(('dp', 'seq'))
- new_decay: float32 [16], replicated
- new_bias: float32 [16], replicated
- new_skip: float32 [16], replicated
- new_gain: float32 [1024], replicated
Inputs may be any that keep to these rules, and one draw needn't show every extreme that they name: `token_ids`: in each sequence exactly one position, never the first, holds id 0.
All inputs are finite; a program needn't handle non-finite values.
Results may differ from a plain program's by a relative error of at most 0.0003.
Values may be sent and summed in bfloat16 or wider, within the bound.
A program may use at most 192 MiB of HBM per device.

v0:
```python
import functools

import jax
import jax.numpy as jnp
from jax import lax
from jax.experimental import pallas as pl
from jax.experimental.pallas import tpu as pltpu
from jax.sharding import PartitionSpec as P

STEPS = 2
norm_floor = 1.0
clip_limit = 1.0
learn_rate = 8.0
highest = lax.Precision.HIGHEST
f32 = jnp.float32
bf16 = jnp.bfloat16
LANES = 128
VMEM = pl.BlockSpec(memory_space=pltpu.VMEM)
SMEM = pl.BlockSpec(memory_space=pltpu.SMEM)
MESH = pl.DeviceIdType.MESH
LIMIT = 60 * 1024 * 1024


def dot(a, b, **kw):
    return jnp.dot(a, b, preferred_element_type=f32, **kw)


def spread_matrix(heads, width):
    size = width // heads
    lane = lax.broadcasted_iota(jnp.int32, (heads, width), 1)
    head = lax.broadcasted_iota(jnp.int32, (heads, width), 0)
    return ((lane >= head * size) & (lane < (head + 1) * size)).astype(bf16)


def split(a):
    high = a.astype(bf16)
    return high, (a - high.astype(f32)).astype(bf16)


def spread(a, ones):
    high, low = split(a)
    return dot(high, ones) + dot(low, ones)


def head_sum(a, ones):
    high, low = split(a)
    turn = (((1,), (1,)), ((), ()))
    one = functools.partial(
        lax.dot_general, dimension_numbers=turn, preferred_element_type=f32
    )
    return one(high, ones) + one(low, ones)


def column(row):
    n = row.shape[1]
    i = lax.broadcasted_iota(jnp.int32, (n, n), 0)
    j = lax.broadcasted_iota(jnp.int32, (n, n), 1)
    return jnp.sum(jnp.where(i == j, row, 0.0), axis=1, keepdims=True)


def gain_rows(width):
    return width // LANES


def state_part(
    pack, raw_t, ids_r, x, proj, sums, sums_t, width, seg_c, seg_r, state, carry
):
    heads, tokens = raw_t.shape
    inner = x.shape[1]
    g = gain_rows(inner)
    ones = spread_matrix(heads, inner)
    rate_row = -jnp.exp(pack[g : g + 1, :heads])
    bias_row = pack[g + 1 : g + 2, :heads]
    w = jax.nn.softplus(raw_t[...].T + bias_row)
    w_t = jax.nn.softplus(raw_t[...] + column(bias_row))
    i = lax.broadcasted_iota(jnp.int32, (tokens, tokens), 0)
    j = lax.broadcasted_iota(jnp.int32, (tokens, tokens), 1)
    lower = (i >= j).astype(f32)
    upper = (i <= j).astype(f32)
    s = dot(lower, w * rate_row, precision=highest)
    sums[...] = s
    sums_t[...] = dot(w_t * column(rate_row), upper, precision=highest)
    width[...] = w
    stop = jnp.where(ids_r[...] == 0, 1.0, 0.0)
    sc = jnp.sum(jnp.where(i >= j, stop, 0.0), axis=1, keepdims=True)
    sr = jnp.sum(jnp.where(i <= j, column(stop), 0.0), axis=0, keepdims=True)
    seg_c[...] = sc
    seg_r[...] = sr
    last = sc[tokens - 1 : tokens, :]
    final = s[tokens - 1 : tokens, :]
    tail = jnp.where(sc == last, jnp.exp(final - s), 0.0)
    weighted = (x[...].astype(f32) * spread(w * tail, ones)).astype(bf16)
    b = proj[:, : proj.shape[1] // 2]
    ended = lax.dot_general(
        b, weighted, (((0,), (0,)), ((), ())), preferred_element_type=f32
    )
    piece = state.shape[1]
    for p in range(state.shape[0]):
        state[p] = ended[p * piece : (p + 1) * piece].astype(bf16)
    kept = jnp.where(last == 0.0, jnp.exp(final), 0.0)
    carry[...] = spread(jnp.broadcast_to(kept, (8, heads)), ones)[0:1, :]


def mix_kernel(
    n_dp, counts, pack, sums, sums_t, width, seg_c, seg_r, x, z, proj, target, weight, state,
    weight_grad, state_grad, row_dot, col_dot, small, loss,
    scaled, mixed, slope_b, prod,
):
    tokens, heads = sums.shape
    inner = x.shape[1]
    g = gain_rows(inner)
    per = LANES // (inner // heads)
    size = inner // heads
    ones = spread_matrix(heads, inner)
    s = sums[...]
    xf = x[...].astype(f32)
    scaled[...] = (xf * spread(width[...], ones)).astype(bf16)
    i = lax.broadcasted_iota(jnp.int32, (tokens, tokens), 0)
    j = lax.broadcasted_iota(jnp.int32, (tokens, tokens), 1)
    same = seg_c[...] == seg_r[...]
    ns = proj.shape[1] // 2
    b, c = proj[:, :ns], proj[:, ns:]
    turn = functools.partial(lax.dot_general, preferred_element_type=f32)
    scores = jnp.where(same & (i >= j), turn(c, b, (((1,), (1,)), ((), ()))), 0.0)
    entry = spread(jnp.where(seg_c[...] == 0.0, jnp.exp(s), 0.0), ones)
    mixed[...] = dot(c, state[...]) * entry
    lane = lax.broadcasted_iota(jnp.int32, (LANES, LANES), 1)
    for k in range(inner // LANES):
        cols = slice(k * LANES, (k + 1) * LANES)
        for at in range(0, tokens, LANES):
            rows = slice(at, at + LANES)
            end = at + LANES
            total = None
            for p in range(per):
                h = k * per + p
                gap = sums[rows, h : h + 1] - sums_t[h : h + 1, :end]
                grid = (jnp.exp(jnp.minimum(gap, 0.0)) * scores[rows, :end]).astype(bf16)
                part = dot(grid, scaled[:end, cols])
                total = part if total is None else jnp.where(lane < p * size, total, part)
            mixed[rows, cols] += total
    gain = jnp.concatenate([pack[k : k + 1, :] for k in range(g)], axis=1)
    skip = spread(jnp.broadcast_to(pack[g + 2 : g + 3, :heads], (8, heads)), ones)[0:1, :]
    zf = z[...].astype(f32)
    silu = zf * jax.nn.sigmoid(zf)
    gated = (mixed[...] + skip * xf) * silu
    root = lax.rsqrt(jnp.mean(gated * gated, axis=1, keepdims=True) + norm_floor)
    normed = (gated * gain * root).astype(bf16)
    residual = dot(normed, weight[...]) - target[...].astype(f32)
    model = target.shape[1]
    total_count = counts[0]
    for k in range(1, n_dp):
        total_count = total_count + counts[k]
    share = 1.0 / (model * total_count.astype(f32))
    position = lax.axis_index("seq") * tokens + lax.broadcasted_iota(jnp.int32, (tokens, 1), 0)
    scored = jnp.where(position < counts[lax.axis_index("dp")], 1.0, 0.0)
    token_loss = jnp.sum(residual * residual, axis=1, keepdims=True) * scored
    loss[...] = jnp.sum(token_loss, axis=0, keepdims=True) * share
    out_grad = (residual * (2.0 * share * scored)).astype(bf16)
    weight_grad[...] = lax.dot_general(
        normed, out_grad, (((0,), (0,)), ((), ())), preferred_element_type=f32
    ).astype(bf16)
    normed_grad = lax.dot_general(
        out_grad, weight[...], (((1,), (1,)), ((), ())), preferred_element_type=f32
    )
    lifted = normed_grad * gated
    gain_grad = jnp.sum(lifted * root, axis=0, keepdims=True)
    inward = jnp.sum(lifted * gain, axis=1, keepdims=True) * (root * root * root / inner)
    dy = (normed_grad * gain * root - gated * inward) * silu
    small[0:1, :] = gain_grad
    small[1:2, :] = jnp.sum(dy * xf, axis=0, keepdims=True)
    row_dot[...] = head_sum(dy * mixed[...], ones)
    state_grad[...] = turn(c, (entry * dy).astype(bf16), (((0,), (0,)), ((), ()))).astype(bf16)
    slope_b[...] = dy.astype(bf16)
    scores_t = turn(b, c, (((1,), (1,)), ((), ())))
    same_t = (seg_c[...] == seg_r[...]) & (i <= j)
    scores_t = jnp.where(same_t, scores_t, 0.0)
    for k in range(inner // LANES):
        cols = slice(k * LANES, (k + 1) * LANES)
        for at in range(0, tokens, LANES):
            rows = slice(at, at + LANES)
            total = None
            for p in range(per):
                h = k * per + p
                gap = sums_t[h : h + 1, at:] - sums[rows, h : h + 1]
                grid = (jnp.exp(jnp.minimum(gap, 0.0)) * scores_t[rows, at:]).astype(bf16)
                part = dot(grid, slope_b[at:, cols])
                total = part if total is None else jnp.where(lane < p * size, total, part)
            prod[rows, cols] = total * x[rows, cols].astype(f32)
    col_dot[...] = head_sum(prod[...], ones)


def back_part(
    pack, raw_t, sums, width, seg_c, x, proj, after, state, carry, row_dot, col_dot, small, loss,
    out,
):
    tokens, heads = sums.shape
    inner = x.shape[1]
    g = gain_rows(inner)
    ones = spread_matrix(heads, inner)
    s = sums[...]
    w = width[...]
    rate_row = -jnp.exp(pack[g : g + 1, :heads])
    bias_row = pack[g + 1 : g + 2, :heads]
    sc = seg_c[...]
    last = sc[tokens - 1 : tokens, :]
    final = s[tokens - 1 : tokens, :]
    tail = jnp.where(sc == last, jnp.exp(final - s), 0.0)
    after = jnp.concatenate([after[p].astype(f32) for p in range(after.shape[0])], axis=0)
    pulled = head_sum(dot(proj[:, : proj.shape[1] // 2], after.astype(bf16)) * x[...].astype(f32), ones) * tail
    moved = after * state[...].astype(f32)
    both = jnp.concatenate(
        [
            jnp.sum(moved, axis=0, keepdims=True) * carry[...],
            small[1:2, :],
            jnp.zeros((6, inner), f32),
        ],
        axis=0,
    )
    both = head_sum(both, ones)
    col = col_dot[...] + pulled
    d_sums = row_dot[...] - w * col
    d_final = jnp.sum(w * pulled, axis=0, keepdims=True) + both[0:1, :]
    i = lax.broadcasted_iota(jnp.int32, (tokens, tokens), 0)
    j = lax.broadcasted_iota(jnp.int32, (tokens, tokens), 1)
    d_rate = dot((i <= j).astype(f32), d_sums, precision=highest) + d_final
    d_width = (col + rate_row * d_rate) * jax.nn.sigmoid(raw_t[...].T + bias_row)
    out[...] = jnp.zeros(out.shape, f32)
    for k in range(g):
        out[k : k + 1, :] = small[0:1, k * LANES : (k + 1) * LANES]
    out[g : g + 1, :heads] = rate_row * jnp.sum(d_rate * w, axis=0, keepdims=True)
    out[g + 1 : g + 2, :heads] = jnp.sum(d_width, axis=0, keepdims=True)
    out[g + 2 : g + 3, :heads] = both[1:2, :]
    out[g + 3 : g + 4, :] = jnp.broadcast_to(loss[...], (1, LANES))


class Spot:
    def __init__(self, n_dp, n_seq):
        self.n_dp, self.n_seq = n_dp, n_seq
        self.cores = 2 if n_dp % 2 == 0 else 1
        self.ys = n_dp // self.cores
        self.highs = 4 if n_seq % 4 == 0 else n_seq
        self.lows = n_seq // self.highs
        self.dp, self.seq = lax.axis_index("dp"), lax.axis_index("seq")
        self.y, self.core = self.dp // self.cores, self.dp % self.cores
        self.high, self.low = self.seq // self.lows, self.seq % self.lows
        self.me = self.dp * n_seq + self.seq

    def core_peer(self, t):
        return (self.y * self.cores + (self.core + t) % self.cores, self.seq)

    def y_peer(self, t):
        return (((self.y + t) % self.ys) * self.cores + self.core, self.seq)

    def low_peer(self, t):
        return (self.dp, self.high * self.lows + (self.low + t) % self.lows)

    def high_peer(self, t):
        return (self.dp, ((self.high + t) % self.highs) * self.lows + self.low)

    def seq_peer(self, t):
        return (self.dp, (self.seq + t) % self.n_seq)

    def meet(self, with_seq):
        barrier = pltpu.get_barrier_semaphore()
        groups = [(self.cores, self.core_peer), (self.ys, self.y_peer)]
        if with_seq:
            groups.append((self.n_seq, self.seq_peer))
        else:
            groups += [(self.lows, self.low_peer), (self.highs, self.high_peer)]
        for count, peer in groups:
            each(
                count,
                lambda t, peer=peer: pl.semaphore_signal(
                    barrier, inc=1, device_id=peer(t), device_id_type=MESH
                ),
            )
        pl.semaphore_wait(barrier, sum(count - 1 for count, _ in groups))


def each(n, body, first=1):
    def one(t, _):
        body(t)
        return 0

    lax.fori_loop(first, n, one, 0)


def remote(source, target, send, recv, peer):
    return pltpu.make_async_remote_copy(
        src_ref=source,
        dst_ref=target,
        send_sem=send,
        recv_sem=recv,
        device_id=peer,
        device_id_type=MESH,
    )


def gather_kernel(
    n_dp, n_seq, pack, raw_t, ids_r, x, proj, rows,
    sums, sums_t, width, seg_c, seg_r, carry, full, entering, carries,
    state, landed, ready, w_recv, high_send, low_send, y_send, core_send,
    s_send, s_recv, c_send, c_recv, r_send, r_recv,
):
    at = Spot(n_dp, n_seq)
    full[at.me] = rows[...].astype(bf16)
    at.meet(True)
    mine = at.seq
    back = lambda t: (mine + n_seq - t) % n_seq

    def lead(t):
        return remote(carry, carries.at[mine], c_send.at[t], c_recv.at[t], at.seq_peer(t))

    def lead_in(t):
        return remote(carry, carries.at[back(t)], c_send.at[t], c_recv.at[t], at.seq_peer(t))

    def first(t):
        p = (mine + t) % n_seq
        return remote(state.at[p], landed.at[mine], s_send.at[t], s_recv.at[t], at.seq_peer(t))

    def first_in(t):
        p = back(t)
        return remote(state.at[p], landed.at[p], s_send.at[t], s_recv.at[t], at.seq_peer(t))

    def second(t):
        p = (mine + t) % n_seq
        return remote(ready.at[p], entering.at[mine], r_send.at[t], r_recv.at[t], at.seq_peer(t))

    def second_in(t):
        p = back(t)
        return remote(ready.at[p], entering.at[p], r_send.at[t], r_recv.at[t], at.seq_peer(t))

    def push(chunk, send, peer):
        return remote(full.at[chunk], full.at[chunk], send, w_recv.at[chunk], peer)

    def high_edge(t):
        return push(at.me, high_send.at[t], at.high_peer(t))

    def low_edge(t, high):
        chunk = at.dp * n_seq + high * at.lows + at.low
        return push(chunk, low_send.at[t * at.highs + high], at.low_peer(t))

    def y_edge(t, seq):
        return push(at.dp * n_seq + seq, y_send.at[t * n_seq + seq], at.y_peer(t))

    def core_edge(t, y, seq):
        chunk = (y * at.cores + at.core) * n_seq + seq
        return push(chunk, core_send.at[(t * at.ys + y) * n_seq + seq], at.core_peer(t))

    def arrived(chunk):
        push(chunk, high_send.at[0], at.core_peer(1)).wait_recv()

    def onward(y, seq, to_low, to_y):
        if to_low:
            each(at.lows, lambda t: low_edge(t, seq // at.lows).start())
        if to_y:
            each(at.ys, lambda t: y_edge(t, seq).start())
        each(at.cores, lambda t: core_edge(t, y, seq).start())

    def start(t):
        lead(t).start()
        first(t).start()

    each(at.highs, lambda t: high_edge(t).start())
    onward(at.y, at.seq, True, True)
    state_part(
        pack, raw_t, ids_r, x, proj, sums, sums_t, width, seg_c, seg_r, state, carry
    )
    each(n_seq, start)
    carries[mine] = carry[...]
    landed[mine] = state[mine]

    def from_high(t):
        seq = ((at.high + at.highs - t) % at.highs) * at.lows + at.low
        arrived(at.dp * n_seq + seq)
        onward(at.y, seq, True, True)

    each(at.highs, from_high)

    def from_low(t):
        low = (at.low + at.lows - t) % at.lows

        def one(u):
            seq = ((at.high + at.highs - u) % at.highs) * at.lows + low
            arrived(at.dp * n_seq + seq)
            onward(at.y, seq, False, True)

        each(at.highs, one, 0)

    each(at.lows, from_low)

    def arrive(t):
        lead_in(t).wait_recv()
        first_in(t).wait_recv()

    each(n_seq, arrive)
    running = jnp.zeros(state.shape[1:], f32)
    for d in range(n_seq):
        ready[d] = running.astype(bf16)
        if d < n_seq - 1:
            running = carries[d] * running + landed[d].astype(f32)
    each(n_seq, lambda t: second(t).start())
    entering[mine] = ready[mine]

    def from_y(t):
        y = (at.y + at.ys - t) % at.ys

        def one(u):
            high, low = u % at.highs, u // at.highs
            seq = ((at.high + high) % at.highs) * at.lows + (at.low + low) % at.lows
            arrived((y * at.cores + at.core) * n_seq + seq)
            onward(y, seq, False, False)

        each(n_seq, one, 0)

    each(at.ys, from_y)
    each(n_seq, lambda t: second_in(t).wait_recv())

    def from_core(t):
        core = (at.core + t) % at.cores

        def one(k):
            arrived(((k // n_seq) * at.cores + core) * n_seq + k % n_seq)

        each(at.ys * n_seq, one, 0)

    each(at.cores, from_core)

    def sent(t):
        lead(t).wait_send()
        first(t).wait_send()
        second(t).wait_send()

    each(n_seq, sent)
    each(at.highs, lambda t: high_edge(t).wait_send())
    each(at.lows, lambda t: each(at.highs, lambda k: low_edge(t, k).wait_send(), 0))
    each(at.ys, lambda t: each(n_seq, lambda k: y_edge(t, k).wait_send(), 0))
    each(
        at.cores,
        lambda t: each(
            at.ys * n_seq, lambda k: core_edge(t, k // n_seq, k % n_seq).wait_send(), 0
        ),
    )


def scatter_kernel(
    n_dp, n_seq, grad, state, carries, pack, raw_t, sums, width, seg_c, x, proj, entering, carry,
    row_dot, col_dot, small, loss_part, rows, new_pack, new_rows, loss,
    part, leaving, by_core, by_y, by_low, by_high,
    staged, from_core, from_y, from_low, from_high, landed, ready,
    core_send, core_recv, y_send, y_recv, low_send, low_recv, high_send, high_recv,
    s_send, s_recv, r_send, r_recv, send, recv,
):
    at = Spot(n_dp, n_seq)
    at.meet(True)
    mine = at.seq
    back = lambda t: (mine + n_seq - t) % n_seq

    def first(t):
        p = (mine + t) % n_seq
        return remote(state.at[p], landed.at[mine], s_send.at[t], s_recv.at[t], at.seq_peer(t))

    def first_in(t):
        p = back(t)
        return remote(state.at[p], landed.at[p], s_send.at[t], s_recv.at[t], at.seq_peer(t))

    def second(t):
        p = (mine + t) % n_seq
        return remote(ready.at[p], leaving.at[mine], r_send.at[t], r_recv.at[t], at.seq_peer(t))

    def second_in(t):
        p = back(t)
        return remote(ready.at[p], leaving.at[p], r_send.at[t], r_recv.at[t], at.seq_peer(t))

    def core_edge(t, y, seq):
        core = (at.core + t) % at.cores
        k = (t * at.ys + y) * n_seq + seq
        return remote(
            grad.at[(y * at.cores + core) * n_seq + seq], from_core.at[k],
            core_send.at[k], core_recv.at[k], at.core_peer(t),
        )

    def y_edge(t, seq):
        k = t * n_seq + seq
        y = (at.y + t) % at.ys
        return remote(
            staged.at[y * n_seq + seq], from_y.at[k], y_send.at[k], y_recv.at[k], at.y_peer(t)
        )

    def low_edge(t, high):
        k = t * at.highs + high
        seq = high * at.lows + (at.low + t) % at.lows
        return remote(
            staged.at[at.y * n_seq + seq], from_low.at[k],
            low_send.at[k], low_recv.at[k], at.low_peer(t),
        )

    def high_edge(t):
        seq = ((at.high + t) % at.highs) * at.lows + at.low
        return remote(
            staged.at[at.y * n_seq + seq], from_high.at[t],
            high_send.at[t], high_recv.at[t], at.high_peer(t),
        )

    def chip_sum(y, seq):
        acc = grad[(y * at.cores + at.core) * n_seq + seq].astype(f32)
        for t in range(1, at.cores):
            core_edge(t, y, seq).wait_recv()
            acc = acc + from_core[(t * at.ys + y) * n_seq + seq].astype(f32)
        return acc

    def y_sum(seq):
        acc = chip_sum(at.y, seq)
        for t in range(1, at.ys):
            y_edge(t, seq).wait_recv()
            acc = acc + from_y[t * n_seq + seq].astype(f32)
        return acc

    def low_sum(high):
        acc = y_sum(high * at.lows + at.low)
        for t in range(1, at.lows):
            low_edge(t, high).wait_recv()
            acc = acc + from_low[t * at.highs + high].astype(f32)
        return acc

    def order(u):
        low = (at.low + 1 + u // at.highs) % at.lows
        return ((at.high + 1 + u) % at.highs) * at.lows + low

    each(n_seq, lambda t: first(t).start())

    def to_core(t):
        def one(k):
            core_edge(t, (at.y + 1 + k // n_seq) % at.ys, order(k % n_seq)).start()

        each(at.ys * n_seq, one, 0)

    each(at.cores, to_core)
    landed[mine] = state[mine]

    half = n_seq // 2

    def to_y(t, lo, hi):
        y = (at.y + t) % at.ys

        def one(u):
            seq = order(u)
            staged[y * n_seq + seq] = chip_sum(y, seq).astype(bf16)
            y_edge(t, seq).start()

        each(hi, one, lo)

    each(at.ys, lambda t: to_y(t, 0, half))
    each(n_seq, lambda t: first_in(t).wait_recv())
    running = jnp.zeros(state.shape[1:], f32)
    for d in reversed(range(n_seq)):
        ready[d] = running.astype(bf16)
        if d > 0:
            running = carries[d] * running + landed[d].astype(f32)
    each(n_seq, lambda t: second(t).start())
    leaving[mine] = ready[mine]
    each(at.ys, lambda t: to_y(t, half, n_seq))
    each(n_seq, lambda t: second_in(t).wait_recv())
    back_part(
        pack, raw_t, sums, width, seg_c, x, proj, leaving, entering, carry, row_dot, col_dot,
        small, loss_part, part,
    )

    def to_low(t):
        def one(u):
            high = (at.high + 1 + u) % at.highs
            seq = high * at.lows + (at.low + t) % at.lows
            staged[at.y * n_seq + seq] = y_sum(seq).astype(bf16)
            low_edge(t, high).start()

        each(at.highs, one, 0)

    each(at.lows, to_low)

    def to_high(t):
        high = (at.high + t) % at.highs
        staged[at.y * n_seq + high * at.lows + at.low] = low_sum(high).astype(bf16)
        high_edge(t).start()

    each(at.highs, to_high)
    acc = low_sum(at.high)
    for t in range(1, at.highs):
        high_edge(t).wait_recv()
        acc = acc + from_high[t].astype(f32)
    g = gain_rows(x.shape[1])
    square = jnp.sum(jnp.sum(acc * acc, axis=1, keepdims=True), axis=0, keepdims=True)
    place = lax.broadcasted_iota(jnp.int32, part.shape, 0)
    summed = jnp.where(place == g + 4, square, part[...])
    levels = [
        (by_core, at.cores, at.core, at.core_peer),
        (by_y, at.ys, at.y, at.y_peer),
        (by_low, at.lows, at.low, at.low_peer),
        (by_high, at.highs, at.high, at.high_peer),
    ]
    base = 0
    for held, count, digit, peer in levels:
        held[digit] = summed

        def edge(t, slot, held=held, digit=digit, peer=peer, base=base):
            return remote(held.at[digit], held.at[slot], send.at[base + t], recv.at[base + t], peer(t))

        each(count, lambda t: edge(t, digit).start())
        each(count, lambda t: edge(t, (digit + count - t) % count).wait_recv())
        summed = held[0]
        for k in range(1, count):
            summed = summed + held[k]
        each(count, lambda t: edge(t, digit).wait_send())
        base += count
    row = lax.broadcasted_iota(jnp.int32, summed.shape, 0)
    grads = jnp.where(row < g + 3, summed, 0.0)
    lane_sum = jnp.sum(grads * grads, axis=0, keepdims=True)
    norm_square = jnp.sum(lane_sum, axis=1, keepdims=True) + summed[g + 4 : g + 5, 0:1]
    factor = clip_limit / jnp.maximum(jnp.sqrt(norm_square), clip_limit)
    new_pack[...] = pack[...] - learn_rate * factor * grads
    new_rows[...] = rows[...] - learn_rate * factor * acc
    loss[...] = summed[g + 3 : g + 4, :]

    def sent(t):
        first(t).wait_send()
        second(t).wait_send()

    each(n_seq, sent)
    each(at.highs, lambda t: high_edge(t).wait_send())
    each(at.lows, lambda t: each(at.highs, lambda k: low_edge(t, k).wait_send(), 0))
    each(at.ys, lambda t: each(n_seq, lambda k: y_edge(t, k).wait_send(), 0))
    each(
        at.cores,
        lambda t: each(
            at.ys * n_seq, lambda k: core_edge(t, k // n_seq, k % n_seq).wait_send(), 0
        ),
    )


def call(body, outs, scratch=(), collective=None):
    extra = {}
    if collective is not None:
        extra = {"collective_id": collective, "has_side_effects": True}

    def run(*args):
        return pl.pallas_call(
            body,
            out_shape=tuple(jax.ShapeDtypeStruct(*o) for o in outs),
            in_specs=[SMEM if a.ndim == 1 else VMEM for a in args],
            out_specs=tuple([VMEM] * len(outs)),
            scratch_shapes=list(scratch),
            compiler_params=pltpu.CompilerParams(vmem_limit_bytes=LIMIT, **extra),
        )(*args)

    return run


def per_device(
    n_dp,
    n_seq,
    head_inputs,
    gate_inputs,
    state_proj,
    time_steps,
    token_ids,
    token_counts,
    teacher_out,
    out_weight,
    decay_log,
    step_bias,
    skip_gain,
    norm_gain,
):
    n = n_dp * n_seq
    x, z, target, raw = head_inputs[0], gate_inputs[0], teacher_out[0], time_steps[0]
    tokens, inner = x.shape
    ns = state_proj.shape[2] // 2
    heads = decay_log.shape[0]
    model = target.shape[1]
    share = out_weight.shape[0]
    piece = ns // n_seq
    g = gain_rows(inner)
    pack_rows = -(-(g + 5) // 8) * 8
    proj = state_proj[0]
    raw_t = raw.T
    ids_r = token_ids
    wide = lambda a: jnp.pad(a, (0, LANES - heads))[None]
    pack = jnp.concatenate(
        [
            norm_gain.reshape(g, LANES),
            wide(decay_log),
            wide(step_bias),
            wide(skip_gain),
            jnp.zeros((pack_rows - g - 3, LANES), f32),
        ]
    )
    rows = out_weight
    dma = pltpu.SemaphoreType.DMA
    losses = []
    per_head = ((tokens, heads), f32)
    for _ in range(STEPS):
        sums, sums_t, width, seg_c, seg_r, carry, full, entering, carries = call(
            functools.partial(gather_kernel, n_dp, n_seq),
            [
                per_head,
                ((heads, tokens), f32),
                per_head,
                ((tokens, 1), f32),
                ((1, tokens), f32),
                ((1, inner), f32),
                ((n, share, model), bf16),
                ((n_seq, piece, inner), bf16),
                ((n_seq, 1, inner), f32),
            ],
            [pltpu.VMEM((n_seq, piece, inner), bf16)] * 3
            + [
                dma((n,)),
                dma((n_seq,)),
                dma((n_seq * n_seq,)),
                dma((n,)),
                dma((n,)),
            ]
            + [dma((n_seq,))] * 6,
            0,
        )(pack, raw_t, ids_r, x, proj, rows)
        weight = full.reshape(n * share, model)
        entering = entering.reshape(ns, inner)
        weight_grad, state_grad, row_dot, col_dot, small, loss = call(
            functools.partial(mix_kernel, n_dp),
            [
                ((inner, model), bf16),
                ((ns, inner), bf16),
                per_head,
                per_head,
                ((8, inner), f32),
                ((1, 1), f32),
            ],
            [
                pltpu.VMEM((tokens, inner), bf16),
                pltpu.VMEM((tokens, inner), f32),
                pltpu.VMEM((tokens, inner), bf16),
                pltpu.VMEM((tokens, inner), f32),
            ],
        )(
            token_counts, pack, sums, sums_t, width, seg_c, seg_r, x, z, proj, target, weight,
            entering,
        )
        pack, rows, loss_row = call(
            functools.partial(scatter_kernel, n_dp, n_seq),
            [((pack_rows, LANES), f32), ((share, model), f32), ((1, LANES), f32)],
            [pltpu.VMEM((pack_rows, LANES), f32), pltpu.VMEM((n_seq, piece, inner), bf16)]
            + [pltpu.VMEM((k, pack_rows, LANES), f32) for k in (n_dp, n_dp, n_seq, n_seq)]
            + [pltpu.VMEM((n, share, model), bf16)] * 3
            + [pltpu.VMEM((n_seq, share, model), bf16)] * 2
            + [pltpu.VMEM((n_seq, piece, inner), bf16)] * 2
            + [dma((n,))] * 4
            + [dma((n_seq,))] * 8
            + [dma((n,))] * 2,
            1,
        )(
            weight_grad.reshape(n, share, model),
            state_grad.reshape(n_seq, piece, inner),
            carries, pack, raw_t, sums, width, seg_c, x, proj, entering, carry, row_dot, col_dot,
            small, loss, rows,
        )
        losses.append(loss_row[0, 0])
    return (
        jnp.stack(losses),
        rows,
        pack[g, :heads],
        pack[g + 1, :heads],
        pack[g + 2, :heads],
        pack[:g].reshape(inner),
    )


def solution(mesh):
    in_specs = (
        P("dp", "seq", None),
        P("dp", "seq", None),
        P("dp", "seq", None),
        P("dp", "seq", None),
        P("dp", "seq"),
        P(),
        P("dp", "seq", None),
        P(("dp", "seq"), None),
        P(),
        P(),
        P(),
        P(),
    )
    out_specs = (P(), P(("dp", "seq"), None), P(), P(), P(), P())
    return jax.shard_map(
        functools.partial(per_device, mesh.shape["dp"], mesh.shape["seq"]),
        mesh=mesh,
        in_specs=in_specs,
        out_specs=out_specs,
        check_vma=False,
    )
```

profile of v0, /device:TPU:0, one launch (start us, length us, event | category | flops | bytes accessed | tf_op | source)
XLA Modules:
  0.0 183.9 jit_solution(8901713140510250720)
XLA Ops:
  0.6 0.7 pad_bitcast_fusion.2
  1.3 0.7 pad_bitcast_fusion
  2.0 1.9 %concatenate.3.pack = f32[16,128]{1,0:T(8,128)} concatenate(f32[8,128]{1,0:T(8,128)} %bitcast.64, f32[1,128]{1,0:T(1,128)S(1)} %pad_bitcast_fusion.2, f32[1,128]{1,0:T(1,128)S(1)} %get-tuple-element.82, f32[1,128]{1,0:T(1,128)S(1)} %get-tuple-element.81, f32[5,128]{1,0:T(8,128)S(1)} %broadcast_in_dim.15), dimensions={0} | concatenate | bytes 16384 | tf_op jit(solution)/shard_map/concatenate | solution.py:687
  3.8 32.1 %shard_map.163 = (f32[384,16]{1,0:T(8,128)}, f32[16,384]{1,0:T(8,128)}, f32[384,16]{1,0:T(8,128)}, f32[384,1]{1,0:T(8,128)}, f32[1,384]{1,0:T(1,128)}, /*index=5...) custom-call(f32[16,128]{1,0:T(8,128)} %concatenate.3.pack, ...), custom_call_target="tpu_custom_call" | custom-call | tf_op jit(solution)/shard_map/pallas_call | solution.py:645
  35.9 13.3 %shard_map.164 = (bf16[1024,1024]{1,0:T(8,128)(2,1)}, bf16[128,1024]{1,0:T(8,128)(2,1)}, f32[384,16]{1,0:T(8,128)}, f32[384,16]{1,0:T(8,128)}, f32[8,1024]{1,0:T(8,128)}, /*index=5*/f32[1,1]{1,0:T(1,128)}) custom-call(s32[4]{0:T(128)} %counts.3, f32[16,128]{1,0:T(8,128)} %concatenate.3.pack, f32[384,16]{1,0:T(8,128)} %get-tuple-element.42.sums, ...), custom_call_target="tpu_custom_call" | custom-call | tf_op jit(solution)/shard_map/pallas_call | solution.py:645
  49.2 43.7 %shard_map.165 = (f32[16,128]{1,0:T(8,128)}, f32[32,1024]{1,0:T(8,128)}, f32[1,128]{1,0:T(1,128)}) custom-call(bf16[32,32,1024]{2,1,0:T(8,128)(2,1)} %bitcast.53, bf16[8,16,1024]{2,1,0:T(8,128)(2,1)} %bitcast.63, f32[8,1,1024]{2,1,0:T(1,128)} %get-tuple-element.51.carries, f32[16,128]{1,0:T(8,128)} %concatenate.3.pack, f32[16,384]{1,0:T(8,128)} %bitcast.59, ...), custom_call_target="tpu_custom_call" | custom-call | tf_op jit(solution)/shard_map/pallas_call | solution.py:645
  92.9 27.3 %shard_map.166 = (f32[384,16]{1,0:T(8,128)}, f32[16,384]{1,0:T(8,128)}, f32[384,16]{1,0:T(8,128)}, f32[384,1]{1,0:T(8,128)}, f32[1,384]{1,0:T(1,128)}, /*index=5...) custom-call(f32[16,128]{1,0:T(8,128)} %get-tuple-element.58.pack, ...), custom_call_target="tpu_custom_call" | custom-call | tf_op jit(solution)/shard_map/pallas_call | solution.py:645
  120.2 13.2 %shard_map.167 = (bf16[1024,1024]{1,0:T(8,128)(2,1)}, bf16[128,1024]{1,0:T(8,128)(2,1)}, f32[384,16]{1,0:T(8,128)}, f32[384,16]{1,0:T(8,128)}, f32[8,1024]{1,0:T(8,128)}, /*index=5*/f32[1,1]{1,0:T(1,128)}) custom-call(s32[4]{0:T(128)} %counts.3, f32[16,128]{1,0:T(8,128)} %get-tuple-element.58.pack, f32[384,16]{1,0:T(8,128)} %get-tuple-element.60.sums, ...), custom_call_target="tpu_custom_call" | custom-call | tf_op jit(solution)/shard_map/pallas_call | solution.py:645
  133.5 0.0 copy-start
  133.5 45.1 %shard_map.168 = (f32[16,128]{1,0:T(8,128)}, f32[32,1024]{1,0:T(8,128)}, f32[1,128]{1,0:T(1,128)}) custom-call(bf16[32,32,1024]{2,1,0:T(8,128)(2,1)} %bitcast.52, bf16[8,16,1024]{2,1,0:T(8,128)(2,1)} %bitcast.62, f32[8,1,1024]{2,1,0:T(1,128)} %get-tuple-element.69.carries, f32[16,128]{1,0:T(8,128)} %get-tuple-element.58.pack, f32[16,384]{1,0:T(8,128)} %bitcast.61, ...), custom_call_target="tpu_custom_call" | custom-call | tf_op jit(solution)/shard_map/pallas_call | solution.py:645
  178.5 0.0 copy-done
  178.6 1.2 pad_maximum_fusion
  179.8 1.3 slice_bitcast_fusion.1
  181.1 1.3 slice_bitcast_fusion
  182.3 1.6 copy.19
  (1 shorter events, 0.0 us)
Async XLA Ops:
  133.5 45.1 %copy-start = (f32[1,128]{1,0:T(1,128)S(1)}, f32[1,128]{1,0:T(1,128)}, u32[]{:S(2)}) copy-start(f32[1,128]{1,0:T(1,128)} %get-tuple-element.57) | copy-start | bytes 1540
where the time goes:
time: 184 us
  Pallas kernels  175 us (95%)
  local copies, waits for them, and re-layouts  7.34 us (4%)
    pallas_call x6, Pallas kernels, run(): pl.pallas_call(body, out_shape=tuple((jax.ShapeDtypeStruct(*o) for o in o...  175 us

commit v1 on v0

v1 whole, which is shorter than its diff:
```python
import functools

import jax
import jax.numpy as jnp
from jax import lax
from jax.experimental import pallas as pl
from jax.experimental.pallas import tpu as pltpu
from jax.sharding import PartitionSpec as P

STEPS = 2
norm_floor = 1.0
clip_limit = 1.0
learn_rate = 8.0
log2e = 1.4426950408889634
f32 = jnp.float32
bf16 = jnp.bfloat16
LANES = 128
VMEM = pl.BlockSpec(memory_space=pltpu.VMEM)
SMEM = pl.BlockSpec(memory_space=pltpu.SMEM)
MESH = pl.DeviceIdType.MESH
LIMIT = 60 * 1024 * 1024


def dot(a, b):
    return jnp.dot(a, b, preferred_element_type=f32)


def contract(a, b, da, db):
    return lax.dot_general(a, b, (((da,), (db,)), ((), ())), preferred_element_type=f32)


def iota(shape, axis):
    return lax.broadcasted_iota(jnp.int32, shape, axis)


def fold(a):
    rows, width = a.shape
    return jnp.sum(a.reshape(rows // 8, 8, width), axis=0)


def total(a):
    return jnp.sum(a, axis=0, keepdims=True)


def lane_total(a):
    return jnp.sum(a, axis=1, keepdims=True)


def flat(a):
    k, rows, width = a.shape
    if rows % 16 == 0 or a.dtype == f32:
        return a.reshape(k * rows, width)
    return a.astype(f32).reshape(k * rows, width).astype(a.dtype)


def each(n, body, first=0):
    if n - first <= 3:
        for t in range(first, n):
            body(t)
        return

    def one(t, _):
        body(t)
        return 0

    lax.fori_loop(first, n, one, 0)


def remote(source, target, send, recv, peer):
    return pltpu.make_async_remote_copy(
        src_ref=source,
        dst_ref=target,
        send_sem=send,
        recv_sem=recv,
        device_id=peer,
        device_id_type=MESH,
    )


class Refs:
    def __init__(self, names, refs):
        self.__dict__.update(zip(names, refs))


class Spot:
    def __init__(self, n_dp, n_seq):
        self.n_dp, self.n_seq, self.n = n_dp, n_seq, n_dp * n_seq
        self.cores = 2 if n_dp % 2 == 0 else 1
        self.ys = n_dp // self.cores
        self.highs = 4 if n_seq % 4 == 0 else n_seq
        self.lows = n_seq // self.highs
        self.dp, self.seq = lax.axis_index("dp"), lax.axis_index("seq")
        self.y, self.core = self.dp // self.cores, self.dp % self.cores
        self.high, self.low = self.seq // self.lows, self.seq % self.lows
        self.me = self.dp * n_seq + self.seq
        y = (self.ys, self.y, self.y_peer)
        x = (self.lows, self.low, self.low_peer)
        self.orders = [(y, x), (x, y)]

    def core_peer(self, t):
        return (self.y * self.cores + (self.core + t) % self.cores, self.seq)

    def y_peer(self, t):
        return (((self.y + t) % self.ys) * self.cores + self.core, self.seq)

    def low_peer(self, t):
        return (self.dp, self.high * self.lows + (self.low + t) % self.lows)

    def high_peer(self, t):
        return (self.dp, ((self.high + t) % self.highs) * self.lows + self.low)

    def seq_peer(self, t):
        return (self.dp, (self.seq + t) % self.n_seq)

    def any_peer(self, t):
        to = (self.me + t) % self.n
        return (to // self.n_seq, to % self.n_seq)

    def plane_peer(self, t):
        to = (self.dp * self.lows + self.low + t) % (self.n_dp * self.lows)
        return (to // self.lows, self.high * self.lows + to % self.lows)

    def split(self, k, first, second):
        return (first, second) if k == 0 else (second, first)

    def seq_at(self, high, low):
        return high * self.lows + low

    def chunk(self, y, seq):
        return (y * self.cores + self.core) * self.n_seq + seq

    def greet(self):
        barrier = pltpu.get_barrier_semaphore()
        each(
            self.n,
            lambda t: pl.semaphore_signal(
                barrier, inc=1, device_id=self.any_peer(t), device_id_type=MESH
            ),
            1,
        )

    def meet(self):
        pl.semaphore_wait(pltpu.get_barrier_semaphore(), self.n - 1)


def to_column(row, k, heads):
    sub, lane = iota((heads, LANES), 0), iota((heads, LANES), 1)
    return lane_total(jnp.where(lane == k * heads + sub, row, 0.0))


def to_row(column, k):
    heads = column.shape[0]
    sub, lane = iota((heads, LANES), 0), iota((heads, LANES), 1)
    return total(jnp.where(lane == k * heads + sub, column, 0.0))


def accumulate(a, upper, axis):
    rows = a.shape[0]
    high = a.astype(bf16)
    rest = a - high.astype(f32)
    mid = rest.astype(bf16)
    low = (rest - mid.astype(f32)).astype(bf16)
    out = contract(jnp.concatenate([high, mid, low], axis=0), upper, 1, axis)
    return out[:rows] + out[rows : 2 * rows] + out[2 * rows :]


class Gather:
    def __init__(self, at, r):
        self.at, self.r = at, r

    def push(self, k, chunk, send, peer):
        r = self.r
        return remote(r.full.at[k, chunk], r.full.at[k, chunk], send, r.w_recv.at[k, chunk], peer)

    def arrived(self, k, chunk):
        self.push(k, chunk, self.r.wz_send.at[k, 0], self.at.core_peer(1)).wait_recv()

    def high_edge(self, k, t):
        return self.push(k, self.at.me, self.r.wz_send.at[k, t], self.at.high_peer(t))

    def inner_edge(self, k, t, high):
        at = self.at
        (_, _, _), (_, _, peer) = at.orders[k]
        chunk = at.chunk(at.y, at.seq_at(high, at.low))
        return self.push(k, chunk, self.r.wi_send.at[k, t * at.highs + high], peer(t))

    def outer_edge(self, k, t, second, high):
        at = self.at
        (_, first, peer), (count, _, _) = at.orders[k]
        y, low = at.split(k, first, second)
        chunk = at.chunk(y, at.seq_at(high, low))
        send = self.r.wo_send.at[k, (t * count + second) * at.highs + high]
        return self.push(k, chunk, send, peer(t))

    def core_edge(self, k, t, y, seq):
        at = self.at
        send = self.r.wc_send.at[k, (t * at.ys + y) * at.n_seq + seq]
        return self.push(k, at.chunk(y, seq), send, at.core_peer(t))

    def onward(self, k, y, low, high, to_inner, to_outer):
        at = self.at
        (outers, _, _), (inners, _, _) = at.orders[k]
        second = low if k == 0 else y
        if to_inner:
            each(inners, lambda t: self.inner_edge(k, t, high).start(), 1)
        if to_outer:
            each(outers, lambda t: self.outer_edge(k, t, second, high).start(), 1)
        each(at.cores, lambda t: self.core_edge(k, t, y, at.seq_at(high, low)).start(), 1)

    def start(self):
        at = self.at
        for k in range(2):
            each(at.highs, lambda t: self.high_edge(k, t).start(), 1)
        for k in range(2):
            self.onward(k, at.y, at.low, at.high, True, True)

    def from_high(self):
        at = self.at

        def one(t):
            high = (at.high + at.highs - t) % at.highs
            for k in range(2):
                self.arrived(k, at.chunk(at.y, at.seq_at(high, at.low)))
                self.onward(k, at.y, at.low, high, True, True)

        each(at.highs, one, 1)

    def from_inner(self):
        at = self.at

        def pick(k, t, u):
            (_, first, _), (count, second, _) = at.orders[k]
            y, low = at.split(k, first, (second + count - t) % count)
            high = (at.high + at.highs - u) % at.highs
            self.arrived(k, at.chunk(y, at.seq_at(high, low)))
            self.onward(k, y, low, high, False, True)

        def both(u):
            for k in range(2):
                each(at.orders[k][1][0], lambda t: pick(k, t, u), 1)

        each(at.highs, both)

    def from_outer(self):
        at = self.at

        def pick(k, t, v):
            (count, first, _), (inners, second, _) = at.orders[k]
            other = (second + v // at.highs) % inners
            high = (at.high + v) % at.highs
            y, low = at.split(k, (first + count - t) % count, other)
            self.arrived(k, at.chunk(y, at.seq_at(high, low)))
            self.onward(k, y, low, high, False, False)

        for k in range(2):
            (count, _, _), (inners, _, _) = at.orders[k]
            each(count, lambda t: each(inners * at.highs, lambda v: pick(k, t, v)), 1)

    def from_core(self):
        at = self.at

        def one(t, v):
            core = (at.core + t) % at.cores
            chunk = ((v // at.n_seq) * at.cores + core) * at.n_seq + v % at.n_seq
            for k in range(2):
                self.arrived(k, chunk)

        each(at.cores, lambda t: each(at.ys * at.n_seq, lambda v: one(t, v)), 1)

    def drain(self):
        at = self.at
        for k in range(2):
            (outers, _, _), (inners, _, _) = at.orders[k]
            each(at.highs, lambda t: self.high_edge(k, t).wait_send(), 1)
            each(
                inners,
                lambda t: each(at.highs, lambda u: self.inner_edge(k, t, u).wait_send()),
                1,
            )
            each(
                outers,
                lambda t: each(
                    inners * at.highs,
                    lambda v: self.outer_edge(k, t, v // at.highs, v % at.highs).wait_send(),
                ),
                1,
            )
            each(
                at.cores,
                lambda t: each(
                    at.ys * at.n_seq,
                    lambda v: self.core_edge(k, t, v // at.n_seq, v % at.n_seq).wait_send(),
                ),
                1,
            )


class Scatter:
    def __init__(self, at, r):
        self.at, self.r = at, r

    def core_edge(self, k, t, y):
        at, r = self.at, self.r
        dp = y * at.cores + (at.core + t) % at.cores
        slot = t * at.ys + y
        return remote(
            r.grad.at[k, pl.ds(dp * at.n_seq, at.n_seq)], r.from_core.at[k, slot],
            r.gc_send.at[k, slot], r.gc_recv.at[k, slot], at.core_peer(t),
        )

    def first_edge(self, k, t, a):
        at, r = self.at, self.r
        (_, _, peer), (count, _, _) = at.orders[k]
        slot = t * count + a
        return remote(
            r.staged1.at[k, slot], r.from1.at[k, slot],
            r.g1_send.at[k, slot], r.g1_recv.at[k, slot], peer(t),
        )

    def second_edge(self, k, t):
        at, r = self.at, self.r
        peer = at.orders[k][1][2]
        return remote(
            r.staged2.at[k, t], r.from2.at[k, t], r.g2_send.at[k, t], r.g2_recv.at[k, t], peer(t)
        )

    def high_edge(self, k, t):
        at, r = self.at, self.r
        return remote(
            r.staged3.at[k, t], r.from3.at[k, t],
            r.g3_send.at[k, t], r.g3_recv.at[k, t], at.high_peer(t),
        )

    def chip_sum(self, k, first, second, high):
        at, r = self.at, self.r
        y, low = at.split(k, first, second)
        seq = at.seq_at(high, low)
        acc = r.grad[k, at.chunk(y, seq)].astype(f32)
        for t in range(1, at.cores):
            acc = acc + r.from_core[k, t * at.ys + y, seq].astype(f32)
        return acc

    def first_sum(self, k, second, high):
        at, r = self.at, self.r
        (firsts, first, _), (count, _, _) = at.orders[k]
        acc = self.chip_sum(k, first, second, high)
        for t in range(1, firsts):
            acc = acc + r.from1[k, t * count + second, high].astype(f32)
        return acc

    def second_sum(self, k, high):
        at, r = self.at, self.r
        _, (count, second, _) = at.orders[k]
        acc = self.first_sum(k, second, high)
        for t in range(1, count):
            acc = acc + r.from2[k, t, high].astype(f32)
        return acc

    def to_first(self):
        at, r = self.at, self.r
        for t in range(1, at.cores):
            for k in range(2):
                each(at.ys, lambda y: self.core_edge(k, t, y).wait_recv())

        def pick(k, t, v):
            (firsts, first, _), (count, second, _) = at.orders[k]
            a = (second + 1 + v) % count

            def one(high):
                acc = self.chip_sum(k, (first + t) % firsts, a, high)
                r.staged1[k, t * count + a, high] = acc.astype(bf16)

            each(at.highs, one)
            self.first_edge(k, t, a).start()

        top = max(order[1][0] for order in at.orders)
        for v in range(top):
            for k in range(2):
                (firsts, _, _), (count, _, _) = at.orders[k]
                if v < count:
                    each(firsts, lambda t: pick(k, t, v), 1)

    def to_second(self):
        at, r = self.at, self.r

        def pick(k, t):
            (firsts, _, _), (count, second, _) = at.orders[k]
            a = (second + t) % count
            each(firsts, lambda u: self.first_edge(k, u, a).wait_recv(), 1)

            def one(high):
                r.staged2[k, t, high] = self.first_sum(k, a, high).astype(bf16)

            each(at.highs, one)
            self.second_edge(k, t).start()

        for k in range(2):
            each(at.orders[k][1][0], lambda t: pick(k, t), 1)

    def to_high(self):
        at, r = self.at, self.r
        for k in range(2):
            (firsts, _, _), (count, second, _) = at.orders[k]
            each(firsts, lambda u: self.first_edge(k, u, second).wait_recv(), 1)
            each(count, lambda t: self.second_edge(k, t).wait_recv(), 1)

            def one(t):
                acc = self.second_sum(k, (at.high + t) % at.highs)
                r.staged3[k, t] = acc.astype(bf16)
                self.high_edge(k, t).start()

            each(at.highs, one, 1)

    def finish(self):
        at, r = self.at, self.r
        half = r.acc.shape[1] // 2
        square = None
        for k in range(2):
            acc = self.second_sum(k, at.high)
            each(at.highs, lambda t: self.high_edge(k, t).wait_recv(), 1)
            for t in range(1, at.highs):
                acc = acc + r.from3[k, t].astype(f32)
            r.acc[:, k * half : (k + 1) * half] = acc
            part = fold(acc * acc)
            square = part if square is None else square + part
        return lane_total(total(square))

    def drain(self):
        at = self.at
        for k in range(2):
            (firsts, _, _), (count, _, _) = at.orders[k]
            for t in range(1, at.cores):
                each(at.ys, lambda y: self.core_edge(k, t, y).wait_send())
            each(
                firsts,
                lambda t: each(count, lambda a: self.first_edge(k, t, a).wait_send()),
                1,
            )
            each(count, lambda t: self.second_edge(k, t).wait_send(), 1)
            each(at.highs, lambda t: self.high_edge(k, t).wait_send(), 1)


class Exchange:
    def __init__(self, at, state, landed, ready, entering, sems):
        self.at, self.state, self.landed, self.ready, self.entering = (
            at, state, landed, ready, entering,
        )
        self.s_send, self.s_recv, self.r_send, self.r_recv = sems

    def back(self, t):
        return (self.at.seq + self.at.n_seq - t) % self.at.n_seq

    def first(self, t):
        p = (self.at.seq + t) % self.at.n_seq
        return remote(
            self.state.at[p], self.landed.at[self.at.seq],
            self.s_send.at[t], self.s_recv.at[t], self.at.seq_peer(t),
        )

    def first_in(self, t):
        p = self.back(t)
        return remote(
            self.state.at[p], self.landed.at[p],
            self.s_send.at[t], self.s_recv.at[t], self.at.seq_peer(t),
        )

    def second(self, t):
        p = (self.at.seq + t) % self.at.n_seq
        return remote(
            self.ready.at[p], self.entering.at[self.at.seq],
            self.r_send.at[t], self.r_recv.at[t], self.at.seq_peer(t),
        )

    def second_in(self, t):
        p = self.back(t)
        return remote(
            self.ready.at[p], self.entering.at[p],
            self.r_send.at[t], self.r_recv.at[t], self.at.seq_peer(t),
        )

    def start(self):
        each(self.at.n_seq, lambda t: self.first(t).start(), 1)
        self.landed[self.at.seq] = self.state[self.at.seq]

    def turn(self, carries, size, order):
        mine, n_seq = self.at.seq, self.at.n_seq
        each(n_seq, lambda t: self.first_in(t).wait_recv(), 1)
        piece, ns = self.state.shape[1:]
        per = piece // size
        for q in range(per):
            rows = slice(q * size, (q + 1) * size)
            running = jnp.zeros((size, ns), f32)
            for n, d in enumerate(order):
                self.ready[d, rows, :] = running.astype(bf16)
                if n < n_seq - 1:
                    kept = carries[d, pl.ds(mine * per + q, 1), :]
                    running = kept * running + self.landed[d, rows, :].astype(f32)
        each(n_seq, lambda t: self.second(t).start(), 1)
        self.entering[mine] = self.ready[mine]

    def finish(self):
        each(self.at.n_seq, lambda t: self.second_in(t).wait_recv(), 1)

    def drain(self):
        each(self.at.n_seq, lambda t: self.first(t).wait_send(), 1)
        each(self.at.n_seq, lambda t: self.second(t).wait_send(), 1)


def train_kernel(n_dp, n_seq, names, *refs):
    r = Refs(names, refs)
    at = Spot(n_dp, n_seq)
    inner, tokens = r.xt.shape
    heads = r.decay.shape[1]
    size = inner // heads
    ns = r.proj.shape[1] // 2
    share, model = r.rows.shape
    half = model // 2
    g = inner // LANES
    blocks = tokens // LANES
    head_rows = [slice(h * size, (h + 1) * size) for h in range(heads)]
    gather, scatter = Gather(at, r), Scatter(at, r)
    fore = Exchange(
        at, r.state, r.landed, r.ready, r.entering, (r.s_send, r.s_recv, r.r_send, r.r_recv)
    )
    rear = Exchange(
        at, r.b_state, r.b_landed, r.b_ready, r.leaving,
        (r.bs_send, r.bs_recv, r.br_send, r.br_recv),
    )
    b, c = slice(0, ns), slice(ns, 2 * ns)

    def wide(column):
        return jnp.concatenate([column] * blocks, axis=1)

    def lead(t):
        return remote(
            r.carries.at[at.seq], r.carries.at[at.seq],
            r.c_send.at[t], r.c_recv.at[t], at.seq_peer(t),
        )

    def lead_in(t):
        p = (at.seq + n_seq - t) % n_seq
        return remote(
            r.carries.at[p], r.carries.at[p], r.c_send.at[t], r.c_recv.at[t], at.seq_peer(t)
        )

    plane = n_dp * at.lows
    place = at.dp * at.lows + at.low

    def plane_edge(t, slot):
        return remote(
            r.gain_a.at[place], r.gain_a.at[slot],
            r.pa_send.at[t], r.pa_recv.at[t], at.plane_peer(t),
        )

    def line_edge(t, slot):
        return remote(
            r.gain_b.at[at.high], r.gain_b.at[slot],
            r.pb_send.at[t], r.pb_recv.at[t], at.high_peer(t),
        )

    at.greet()
    r.held[...] = r.rows[...]
    for k, ref in enumerate((r.decay, r.bias, r.skip)):
        sub, lane = iota((heads, heads), 0), iota((heads, heads), 1)
        own = lane_total(jnp.where(sub == lane, ref[...], 0.0))
        row = to_row(own, k)
        packed = row if k == 0 else packed + row
    r.params[...] = packed
    r.gain_now[...] = r.gain[...]
    r.upper[...] = (iota((tokens, tokens), 0) <= iota((tokens, tokens), 1)).astype(bf16)
    for k in range(g):
        cols = slice(k * LANES, (k + 1) * LANES)
        r.xt[cols, :] = r.x[:, cols].astype(f32).T
    stop = jnp.where(r.ids[...] == 0, 1.0, 0.0)
    r.seg[...] = dot(jnp.broadcast_to(stop, (16, tokens)).astype(bf16), r.upper[...])

    def prepare():
        seg_c = r.seg[...].T[:, 0:1]
        raw = contract(r.proj[:, b], r.proj[:, c], 1, 1)
        open_to = (seg_c == r.seg[0:1, :]) & (
            iota((tokens, tokens), 0) <= iota((tokens, tokens), 1)
        )
        r.score[...] = jnp.where(open_to, raw, 0.0)
        for k in range(g):
            cols = slice(k * LANES, (k + 1) * LANES)
            zt = r.z[:, cols].astype(f32).T
            r.gate[cols, :] = zt * jax.nn.sigmoid(zt)

    def forward_head(h):
        rows = head_rows[h]
        for jb in range(blocks):
            js = slice(jb * LANES, (jb + 1) * LANES)
            left = r.sums_c[js, h : h + 1]
            for ib in range(jb, blocks):
                cs = slice(ib * LANES, (ib + 1) * LANES)
                gap = r.sums[h : h + 1, cs] - left
                if ib == jb:
                    gap = jnp.minimum(gap, 0.0)
                r.grid[h, js, cs] = (jnp.exp2(gap) * r.score[js, cs]).astype(bf16)
        for ib in range(blocks):
            end = (ib + 1) * LANES
            cs = slice(ib * LANES, end)
            r.mixed[rows, cs] = dot(r.scaled[rows, :end], r.grid[h, :end, cs])

    def backward_head(h):
        rows = head_rows[h]
        for jb in range(blocks):
            at_j = jb * LANES
            js = slice(at_j, at_j + LANES)
            part = contract(r.slope[rows, at_j:], r.grid[h, js, at_j:], 1, 1)
            r.col_dot[h : h + 1, js] = total(part * r.xt[rows, js])

    def step(s, _):
        for k in range(2):
            r.full[k, at.me] = r.held[:, k * half : (k + 1) * half].astype(bf16)

        @pl.when(s == 0)
        def _():
            at.meet()

        gather.start()

        packed = r.params[...]
        rate = -jnp.exp(jnp.broadcast_to(to_column(packed, 0, heads), (heads, tokens)))
        bias = jnp.broadcast_to(to_column(packed, 1, heads), (heads, tokens))
        w = jax.nn.softplus(r.raw_t[...] + bias)
        sums = accumulate(w * (rate * log2e), r.upper[...], 0)
        seg = r.seg[...][:heads]
        final = sums[:, tokens - 1 : tokens]
        last = seg[:, tokens - 1 : tokens]
        tail = jnp.where(seg == last, jnp.exp2(final - sums), 0.0)
        r.rate[...] = rate
        r.bias_w[...] = bias
        r.width[...] = w
        r.sums[...] = sums
        r.tail[...] = tail
        r.ending[...] = w * tail
        r.entry[...] = jnp.where(seg == 0.0, jnp.exp2(sums), 0.0)
        r.carries[at.seq] = jnp.broadcast_to(
            jnp.where(last == 0.0, jnp.exp2(final), 0.0), (heads, LANES)
        )
        for h in range(heads):
            rows = head_rows[h]
            r.slope[rows, :] = (r.xt[rows, :] * r.ending[h : h + 1, :]).astype(bf16)
        ended = dot(r.slope[...], r.proj[:, b])
        r.state[...] = ended.reshape(r.state.shape).astype(bf16)
        each(n_seq, lambda t: lead(t).start(), 1)
        fore.start()

        r.sums_c[...] = sums.T
        for h in range(heads):
            rows = head_rows[h]
            r.scaled[rows, :] = (r.xt[rows, :] * r.width[h : h + 1, :]).astype(bf16)

        @pl.when(s == 0)
        def _():
            prepare()

        gather.from_high()
        for k in range(g):
            row = jnp.broadcast_to(r.gain_now[k : k + 1, :], (LANES, LANES))
            r.gain_w[k * LANES : (k + 1) * LANES, :] = row.T
        cut = heads // 4
        for h in range(cut):
            forward_head(h)
        gather.from_inner()
        each(n_seq, lambda t: lead_in(t).wait_recv(), 1)
        fore.turn(r.carries, size, list(range(n_seq)))
        for h in range(cut, 3 * cut):
            forward_head(h)
        gather.from_outer()
        for h in range(3 * cut, heads):
            forward_head(h)
        fore.finish()

        passed = contract(flat(r.entering[...]), r.proj[:, c], 1, 1)
        skip = jnp.broadcast_to(to_column(packed, 2, heads), (heads, tokens))
        r.skip_w[...] = skip
        power = jnp.zeros((8, tokens), f32)
        for h in range(heads):
            rows = head_rows[h]
            y = r.mixed[rows, :] + passed[rows, :] * r.entry[h : h + 1, :]
            r.mixed[rows, :] = y
            gated = (y + r.skip_w[h : h + 1, :] * r.xt[rows, :]) * r.gate[rows, :]
            r.gated[rows, :] = gated
            power = power + fold(gated * gated)
        root = lax.rsqrt(total(power) * (1.0 / inner) + norm_floor)
        r.root[...] = jnp.broadcast_to(root, r.root.shape)
        for k in range(g):
            rows = slice(k * LANES, (k + 1) * LANES)
            normed = r.gated[rows, :] * wide(r.gain_w[rows, :]) * r.root[0:1, :]
            r.normed[rows, :] = normed.astype(bf16)
            r.normed_n[:, rows] = normed.T.astype(bf16)

        gather.from_core()
        for k in range(2):
            r.residual[:, k * half : (k + 1) * half] = dot(r.normed_n[...], flat(r.full[k]))
        count = r.counts[0]
        for k in range(1, n_dp):
            count = count + r.counts[k]
        share_of = 1.0 / (model * count.astype(f32))
        limit = r.counts[at.dp] - at.seq * tokens
        lost = jnp.zeros((8, model), f32)
        step_rows = 32
        for q in range(tokens // step_rows):
            rows = slice(q * step_rows, (q + 1) * step_rows)
            scored = iota((step_rows, model), 0) + q * step_rows < limit
            gap = jnp.where(scored, r.residual[rows, :] - r.target[rows, :].astype(f32), 0.0)
            lost = lost + fold(gap * gap)
            r.og[rows, :] = (gap * (2.0 * share_of)).astype(bf16)
        loss = lane_total(total(lost)) * share_of

        def weight_part(t, y):
            dp = y * at.cores + (at.core + t) % at.cores
            width = n_seq * share
            left = r.normed[pl.ds(pl.multiple_of(dp * width, width), width), :]
            for k in range(2):
                out = dot(left, r.og[:, k * half : (k + 1) * half])
                r.grad[k, pl.ds(dp * n_seq, n_seq)] = out.reshape(n_seq, share, half).astype(bf16)
                if t > 0:
                    scatter.core_edge(k, t, y).start()

        for t in range(1, at.cores):
            for u in range(at.ys):
                weight_part(t, (at.y + 1 + u) % at.ys)
        r.ng[...] = contract(flat(r.full[0]), r.og[:, :half], 1, 1)
        r.ng[...] += contract(flat(r.full[1]), r.og[:, half:], 1, 1)
        inward = jnp.zeros((8, tokens), f32)
        for h in range(heads):
            rows = head_rows[h]
            lifted = r.ng[rows, :] * r.gated[rows, :]
            inward = inward + fold(lifted * wide(r.gain_w[rows, :]))
            lifted = lifted * r.root[0:1, :]
            part = lifted[:, :LANES]
            for k in range(1, blocks):
                part = part + lifted[:, k * LANES : (k + 1) * LANES]
            r.gain_part[rows, :] = part
        root = r.root[0:1, :]
        inward = total(inward) * (root * root * root * (1.0 / inner))
        r.inward[...] = jnp.broadcast_to(inward, r.inward.shape)
        for h in range(heads):
            rows = head_rows[h]
            dy = r.ng[rows, :] * wide(r.gain_w[rows, :]) * r.root[0:1, :]
            dy = (dy - r.gated[rows, :] * r.inward[0:1, :]) * r.gate[rows, :]
            r.row_dot[h : h + 1, :] = total(dy * r.mixed[rows, :])
            r.skip_dot[h : h + 1, :] = total(dy * r.xt[rows, :])
            r.slope[rows, :] = dy.astype(bf16)
            r.scaled[rows, :] = (dy * r.entry[h : h + 1, :]).astype(bf16)
        pulled = dot(r.scaled[...], r.proj[:, c])
        r.b_state[...] = pulled.reshape(r.b_state.shape).astype(bf16)
        rear.start()
        for u in range(at.ys):
            weight_part(0, (at.y + 1 + u) % at.ys)
        for k in range(g):
            rows = slice(k * LANES, (k + 1) * LANES)
            r.gain_a[place, k : k + 1, :] = total(r.gain_part[rows, :].T)
        each(plane, lambda t: plane_edge(t, place).start(), 1)
        scatter.to_first()
        for h in range(cut):
            backward_head(h)
        rear.turn(r.carries, size, list(reversed(range(n_seq))))
        for h in range(cut, 3 * cut):
            backward_head(h)
        scatter.to_second()
        for h in range(3 * cut, heads):
            backward_head(h)
        each(plane, lambda t: plane_edge(t, (place + plane - t) % plane).wait_recv(), 1)
        gain_sum = r.gain_a[0]
        for k in range(1, plane):
            gain_sum = gain_sum + r.gain_a[k]
        r.gain_b[at.high] = gain_sum
        each(at.highs, lambda t: line_edge(t, at.high).start(), 1)
        scatter.to_high()
        gather.drain()
        rear.finish()

        after = flat(r.leaving[...])
        moved = contract(after, r.proj[:, b], 1, 1)
        for h in range(heads):
            rows = head_rows[h]
            r.pulled[h : h + 1, :] = total(moved[rows, :] * r.xt[rows, :])
        piece = r.leaving.shape[1]
        for h in range(heads):
            p, q = (h * size) // piece, (h * size) % piece
            own = r.leaving[p, q : q + size, :].astype(f32)
            own = own * r.entering[p, q : q + size, :].astype(f32)
            r.kept[h : h + 1, :] = total(own)
        drawn = r.pulled[...] * r.tail[...]
        w, rate = r.width[...], r.rate[...]
        col = r.col_dot[...] + drawn
        d_final = lane_total(w * drawn) + lane_total(r.kept[...] * r.carries[at.seq])
        d_rate = accumulate(r.row_dot[...] - w * col, r.upper[...], 1) + d_final
        d_width = (col + rate * d_rate) * jax.nn.sigmoid(r.raw_t[...] + r.bias_w[...])
        message = (
            to_row(lane_total(rate * d_rate * w), 0)
            + to_row(lane_total(d_width), 1)
            + to_row(lane_total(r.skip_dot[...]), 2)
        )
        square = scatter.finish()
        lane = iota((1, LANES), 1)
        message = message + jnp.where(lane == 3 * heads, loss, 0.0)
        message = message + jnp.where(lane == 3 * heads + 1, square, 0.0)
        r.inbox[s, at.me] = message

        def news(t, slot):
            return remote(
                r.inbox.at[s, at.me], r.inbox.at[s, slot],
                r.n_send.at[t], r.n_recv.at[t], at.any_peer(t),
            )

        each(at.n, lambda t: news(t, at.me).start(), 1)
        each(at.highs, lambda t: line_edge(t, (at.high + at.highs - t) % at.highs).wait_recv(), 1)
        gain_sum = r.gain_b[0]
        for k in range(1, at.highs):
            gain_sum = gain_sum + r.gain_b[k]
        scatter.drain()
        fore.drain()
        rear.drain()
        each(n_seq, lambda t: lead(t).wait_send(), 1)
        each(plane, lambda t: plane_edge(t, place).wait_send(), 1)
        each(at.highs, lambda t: line_edge(t, at.high).wait_send(), 1)
        each(at.n, lambda t: news(t, (at.me + at.n - t) % at.n).wait_recv(), 1)
        each(at.n, lambda t: news(t, at.me).wait_send(), 1)
        sums = jnp.sum(r.inbox[s], axis=0)
        small = jnp.where(lane < 3 * heads, sums, 0.0)
        norm = lane_total(small * small + total(gain_sum * gain_sum))
        norm = norm + lane_total(jnp.where(lane == 3 * heads + 1, sums, 0.0))
        pace = learn_rate * clip_limit / jnp.maximum(jnp.sqrt(norm), clip_limit)
        r.params[...] = r.params[...] - pace * small
        r.gain_now[...] = r.gain_now[...] - pace * gain_sum
        r.held[...] = r.held[...] - pace * r.acc[...]
        r.out_small[pl.ds(s + 1, 1), :] = jnp.broadcast_to(
            lane_total(jnp.where(lane == 3 * heads, sums, 0.0)), (1, LANES)
        )
        return 0

    lax.fori_loop(0, STEPS, step, 0)
    r.out_small[0:1, :] = r.params[...]
    r.out_gain[...] = r.gain_now[...]
    r.out_rows[...] = r.held[...]


def finish_kernel(rows, small, gain, losses, new_rows, decay, bias, skip, new_gain):
    heads = decay.shape[1]
    new_rows[...] = rows[...]
    new_gain[...] = gain[...]
    for k, ref in enumerate((decay, bias, skip)):
        ref[...] = small[0:1, k * heads : (k + 1) * heads]
    lane = iota((1, LANES), 1)
    both = jnp.where(lane == 0, small[1:2, :], small[2:3, :])
    losses[...] = both[:, :STEPS]


def call(body, outs, args, scratch=(), **extra):
    return pl.pallas_call(
        body,
        out_shape=tuple(jax.ShapeDtypeStruct(*o) for o in outs),
        in_specs=[SMEM if a.ndim == 1 else VMEM for a in args],
        out_specs=tuple([VMEM] * len(outs)),
        scratch_shapes=list(scratch),
        compiler_params=pltpu.CompilerParams(vmem_limit_bytes=LIMIT, **extra),
    )(*args)


def per_device(
    n_dp,
    n_seq,
    head_inputs,
    gate_inputs,
    state_proj,
    time_steps,
    token_ids,
    token_counts,
    teacher_out,
    out_weight,
    decay_log,
    step_bias,
    skip_gain,
    norm_gain,
):
    n = n_dp * n_seq
    x, z, target, raw = head_inputs[0], gate_inputs[0], teacher_out[0], time_steps[0]
    tokens, inner = x.shape
    ns = state_proj.shape[2] // 2
    heads = decay_log.shape[0]
    model = target.shape[1]
    half = model // 2
    share = out_weight.shape[0]
    piece = inner // n_seq
    g = inner // LANES
    cores = 2 if n_dp % 2 == 0 else 1
    ys = n_dp // cores
    highs = 4 if n_seq % 4 == 0 else n_seq
    lows = n_seq // highs
    most = max(ys, lows)
    per_head, tall = ((heads, tokens), f32), (inner, tokens)
    state = ((n_seq, piece, ns), bf16)
    dma = pltpu.SemaphoreType.DMA
    vmem = {
        "xt": (tall, f32),
        "gate": (tall, f32),
        "mixed": (tall, f32),
        "gated": (tall, f32),
        "ng": (tall, f32),
        "scaled": (tall, bf16),
        "slope": (tall, bf16),
        "normed": (tall, bf16),
        "normed_n": ((tokens, inner), bf16),
        "residual": ((tokens, model), f32),
        "og": ((tokens, model), bf16),
        "upper": ((tokens, tokens), bf16),
        "score": ((tokens, tokens), f32),
        "grid": ((heads, tokens, tokens), bf16),
        "seg": ((16, tokens), f32),
        "sums_c": ((tokens, heads), f32),
        "rate": per_head,
        "bias_w": per_head,
        "skip_w": per_head,
        "width": per_head,
        "sums": per_head,
        "tail": per_head,
        "ending": per_head,
        "entry": per_head,
        "row_dot": per_head,
        "skip_dot": per_head,
        "col_dot": per_head,
        "pulled": per_head,
        "kept": ((heads, ns), f32),
        "root": ((8, tokens), f32),
        "inward": ((8, tokens), f32),
        "gain_w": ((inner, LANES), f32),
        "gain_part": ((inner, LANES), f32),
        "gain_now": ((g, LANES), f32),
        "params": ((1, LANES), f32),
        "held": ((share, model), f32),
        "acc": ((share, model), f32),
        "full": ((2, n, share, half), bf16),
        "grad": ((2, n, share, half), bf16),
        "from_core": ((2, cores * ys, n_seq, share, half), bf16),
        "staged1": ((2, most * most, highs, share, half), bf16),
        "from1": ((2, most * most, highs, share, half), bf16),
        "staged2": ((2, most, highs, share, half), bf16),
        "from2": ((2, most, highs, share, half), bf16),
        "staged3": ((2, highs, share, half), bf16),
        "from3": ((2, highs, share, half), bf16),
        "state": state,
        "landed": state,
        "ready": state,
        "entering": state,
        "b_state": state,
        "b_landed": state,
        "b_ready": state,
        "leaving": state,
        "carries": ((n_seq, heads, LANES), f32),
        "gain_a": ((n_dp * lows, g, LANES), f32),
        "gain_b": ((highs, g, LANES), f32),
        "inbox": ((STEPS, n, 1, LANES), f32),
    }
    sems = {
        "w_recv": (2, n),
        "wz_send": (2, highs),
        "wi_send": (2, most * highs),
        "wo_send": (2, most * most * highs),
        "wc_send": (2, cores * ys * n_seq),
        "gc_send": (2, cores * ys),
        "gc_recv": (2, cores * ys),
        "g1_send": (2, most * most),
        "g1_recv": (2, most * most),
        "g2_send": (2, most),
        "g2_recv": (2, most),
        "g3_send": (2, highs),
        "g3_recv": (2, highs),
        "pa_send": (n_dp * lows,),
        "pa_recv": (n_dp * lows,),
        "pb_send": (highs,),
        "pb_recv": (highs,),
        "n_send": (n,),
        "n_recv": (n,),
    }
    for name in ("c", "s", "r", "bs", "br"):
        sems[name + "_send"] = (n_seq,)
        sems[name + "_recv"] = (n_seq,)
    given = {
        "counts": token_counts,
        "decay": decay_log.reshape(1, heads),
        "bias": step_bias.reshape(1, heads),
        "skip": skip_gain.reshape(1, heads),
        "gain": norm_gain.reshape(g, LANES),
        "raw_t": raw.T,
        "ids": token_ids,
        "x": x,
        "z": z,
        "target": target,
        "proj": state_proj[0],
        "rows": out_weight,
    }
    outs = {
        "out_rows": ((share, model), f32),
        "out_small": ((8, LANES), f32),
        "out_gain": ((g, LANES), f32),
    }
    names = [*given, *outs, *vmem, *sems]
    rows, small, gain = call(
        functools.partial(train_kernel, n_dp, n_seq, names),
        outs.values(),
        tuple(given.values()),
        [pltpu.VMEM(*v) for v in vmem.values()] + [dma(v) for v in sems.values()],
        collective_id=0,
        has_side_effects=True,
    )
    losses, rows, decay, bias, skip, gain = call(
        finish_kernel,
        [
            ((1, STEPS), f32),
            ((share, model), f32),
            ((1, heads), f32),
            ((1, heads), f32),
            ((1, heads), f32),
            ((g, LANES), f32),
        ],
        (rows, small, gain),
    )
    return (
        losses.reshape(STEPS),
        rows,
        decay.reshape(heads),
        bias.reshape(heads),
        skip.reshape(heads),
        gain.reshape(inner),
    )


def solution(mesh):
    in_specs = (
        P("dp", "seq", None),
        P("dp", "seq", None),
        P("dp", "seq", None),
        P("dp", "seq", None),
        P("dp", "seq"),
        P(),
        P("dp", "seq", None),
        P(("dp", "seq"), None),
        P(),
        P(),
        P(),
        P(),
    )
    out_specs = (P(), P(("dp", "seq"), None), P(), P(), P(), P())
    return jax.shard_map(
        functools.partial(per_device, mesh.shape["dp"], mesh.shape["seq"]),
        mesh=mesh,
        in_specs=in_specs,
        out_specs=out_specs,
        check_vma=False,
    )
```

time: 184 us -> 123 us (0.67)
  Pallas kernels: 175 us -> 122 us
  local copies, waits for them, and re-layouts: 7.34 us -> 0 us
    pallas_call x6 -> x2, Pallas kernels: 175 us -> 122 us  [call(): pl.pallas_call(body, out_shape=tuple((jax.ShapeDtypeStruct(*o) for o in o...]
    concatenate x1 -> x0, local copies, waits for them, and re-layouts: 1.87 us -> none  [per_device(): jnp.concatenate([norm_gain.reshape(g, LANES), wide(decay_log), wide(step_...]
where the time goes in v1:
time: 123 us
  Pallas kernels  122 us (99%)
    pallas_call x2, Pallas kernels, call(): pl.pallas_call(body, out_shape=tuple((jax.ShapeDtypeStruct(*o) for o in o...  122 us

profile of v1, /device:TPU:0, one launch (start us, length us, event | category | flops | bytes accessed | tf_op | source)
XLA Modules:
  0.0 122.7 jit_solution(9551553937781242616)
XLA Ops:
  0.6 120.5 %shard_map.163 = (f32[32,1024]{1,0:T(8,128)}, f32[8,128]{1,0:T(8,128)}, f32[8,128]{1,0:T(8,128)}) custom-call(s32[4]{0:T(128)} %refs_0_.1, f32[1,16]{1,0:T(1,128)} %bitcast.22, f32[1,16]{1,0:T(1,128)} %bitcast.23, f32[1,16]{1,0:T(1,128)} %bitcast.24, f32[8,128]{1,0:T(8,128)} %bitcast.21, f32[16,384]{1,0:T(8,128)} %bitcast.20, s32[1,384]{1,0:T(1,128)} %refs_6_.1, ...), custom_call_target="tpu_custom_call" | custom-call | tf_op jit(solution)/shard_map/pallas_call | solution.py:855
  121.1 1.6 %shard_map.164 = (f32[1,2]{1,0:T(1,128)}, f32[32,1024]{1,0:T(8,128)}, f32[1,16]{1,0:T(1,128)}, f32[1,16]{1,0:T(1,128)}, f32[1,16]{1,0:T(1,128)}, /*index=5*/f32[8,128]{1,0:T(8,128)}) custom-call(f32[32,1024]{1,0:T(8,128)} %get-tuple-element.15.rows, f32[8,128]{1,0:T(8,128)} %get-tuple-element.16.small, f32[8,128]{1,0:T(8,128)} %get-tuple-element.17.gain), custom_call_target="tpu_custom_call" | custom-call | tf_op jit(solution)/shard_map/pallas_call | solution.py:855

commit v2 on v1

v2 whole, which is shorter than its diff:
```python
import functools

import jax
import jax.numpy as jnp
from jax import lax
from jax.experimental import pallas as pl
from jax.experimental.pallas import tpu as pltpu
from jax.sharding import PartitionSpec as P

STEPS = 2
norm_floor = 1.0
clip_limit = 1.0
learn_rate = 8.0
log2e = 1.4426950408889634
f32 = jnp.float32
bf16 = jnp.bfloat16
LANES = 128
VMEM = pl.BlockSpec(memory_space=pltpu.VMEM)
SMEM = pl.BlockSpec(memory_space=pltpu.SMEM)
MESH = pl.DeviceIdType.MESH
LIMIT = 60 * 1024 * 1024


def dot(a, b):
    return jnp.dot(a, b, preferred_element_type=f32)


def contract(a, b, da, db):
    return lax.dot_general(a, b, (((da,), (db,)), ((), ())), preferred_element_type=f32)


def iota(shape, axis):
    return lax.broadcasted_iota(jnp.int32, shape, axis)


def fold(a):
    rows, width = a.shape
    return jnp.sum(a.reshape(rows // 8, 8, width), axis=0)


def total(a):
    return jnp.sum(a, axis=0, keepdims=True)


def lane_total(a):
    return jnp.sum(a, axis=1, keepdims=True)


def flat(a):
    k, rows, width = a.shape
    if rows % 16 == 0 or a.dtype == f32:
        return a.reshape(k * rows, width)
    return a.astype(f32).reshape(k * rows, width).astype(a.dtype)


def each(n, body, first=0):
    if n - first <= 3:
        for t in range(first, n):
            body(t)
        return

    def one(t, _):
        body(t)
        return 0

    lax.fori_loop(first, n, one, 0)


def remote(source, target, send, recv, peer):
    return pltpu.make_async_remote_copy(
        src_ref=source,
        dst_ref=target,
        send_sem=send,
        recv_sem=recv,
        device_id=peer,
        device_id_type=MESH,
    )


class Refs:
    def __init__(self, names, refs):
        self.__dict__.update(zip(names, refs))


class Spot:
    def __init__(self, n_dp, n_seq):
        self.n_dp, self.n_seq, self.n = n_dp, n_seq, n_dp * n_seq
        self.cores = 2 if n_dp % 2 == 0 else 1
        self.ys = n_dp // self.cores
        self.highs = 4 if n_seq % 4 == 0 else n_seq
        self.lows = n_seq // self.highs
        self.dp, self.seq = lax.axis_index("dp"), lax.axis_index("seq")
        self.y, self.core = self.dp // self.cores, self.dp % self.cores
        self.high, self.low = self.seq // self.lows, self.seq % self.lows
        self.me = self.dp * n_seq + self.seq
        self.group = n_seq // 2
        self.part, self.spot = self.seq // self.group, self.seq % self.group

    def core_peer(self, t):
        return (self.y * self.cores + (self.core + t) % self.cores, self.seq)

    def y_peer(self, t):
        return (((self.y + t) % self.ys) * self.cores + self.core, self.seq)

    def low_peer(self, t):
        return (self.dp, self.high * self.lows + (self.low + t) % self.lows)

    def high_peer(self, t):
        return (self.dp, ((self.high + t) % self.highs) * self.lows + self.low)

    def group_peer(self, t):
        return (self.dp, self.part * self.group + (self.spot + t) % self.group)

    def other_half(self):
        return (self.dp, (self.seq + self.group) % self.n_seq)

    def any_peer(self, t):
        to = (self.me + t) % self.n
        return (to // self.n_seq, to % self.n_seq)

    def plane_peer(self, t):
        to = (self.dp * self.lows + self.low + t) % (self.n_dp * self.lows)
        return (to // self.lows, self.high * self.lows + to % self.lows)

    def chunk(self, y, high, low):
        return (y * self.cores + self.core) * self.n_seq + high * self.lows + low

    def greet(self):
        barrier = pltpu.get_barrier_semaphore()
        each(
            self.n,
            lambda t: pl.semaphore_signal(
                barrier, inc=1, device_id=self.any_peer(t), device_id_type=MESH
            ),
            1,
        )

    def meet(self):
        pl.semaphore_wait(pltpu.get_barrier_semaphore(), self.n - 1)


def to_column(row, k, heads):
    sub, lane = iota((heads, LANES), 0), iota((heads, LANES), 1)
    return lane_total(jnp.where(lane == k * heads + sub, row, 0.0))


def to_row(column, k):
    heads = column.shape[0]
    sub, lane = iota((heads, LANES), 0), iota((heads, LANES), 1)
    return total(jnp.where(lane == k * heads + sub, column, 0.0))


def accumulate(a, upper, axis):
    rows = a.shape[0]
    high = a.astype(bf16)
    rest = a - high.astype(f32)
    mid = rest.astype(bf16)
    low = (rest - mid.astype(f32)).astype(bf16)
    out = contract(jnp.concatenate([high, mid, low], axis=0), upper, 1, axis)
    return out[:rows] + out[rows : 2 * rows] + out[2 * rows :]


class Gather:
    def __init__(self, at, r):
        self.at, self.r = at, r

    def push(self, chunk, send, peer):
        r = self.r
        return remote(r.full.at[chunk], r.full.at[chunk], send, r.w_recv.at[chunk], peer)

    def arrived(self, chunk):
        self.push(chunk, self.r.wz_send.at[0], self.at.core_peer(1)).wait_recv()

    def high_edge(self, t):
        return self.push(self.at.me, self.r.wz_send.at[t], self.at.high_peer(t))

    def low_edge(self, t, high):
        at = self.at
        chunk = at.chunk(at.y, high, at.low)
        return self.push(chunk, self.r.wx_send.at[t * at.highs + high], at.low_peer(t))

    def y_edge(self, t, high, low):
        at = self.at
        send = self.r.wy_send.at[(t * at.highs + high) * at.lows + low]
        return self.push(at.chunk(at.y, high, low), send, at.y_peer(t))

    def core_edge(self, t, y, seq):
        at = self.at
        send = self.r.wc_send.at[(t * at.ys + y) * at.n_seq + seq]
        return self.push((y * at.cores + at.core) * at.n_seq + seq, send, at.core_peer(t))

    def onward(self, y, high, low, to_low, to_y):
        at = self.at
        if to_low:
            each(at.lows, lambda t: self.low_edge(t, high).start(), 1)
        if to_y:
            each(at.ys, lambda t: self.y_edge(t, high, low).start(), 1)
        each(at.cores, lambda t: self.core_edge(t, y, high * at.lows + low).start(), 1)

    def start(self):
        at = self.at
        each(at.highs, lambda t: self.high_edge(t).start(), 1)
        self.onward(at.y, at.high, at.low, True, True)

    def from_high(self):
        at = self.at

        def one(t):
            high = (at.high + at.highs - t) % at.highs
            self.arrived(at.chunk(at.y, high, at.low))
            self.onward(at.y, high, at.low, True, True)

        each(at.highs, one, 1)

    def from_low(self, u):
        at = self.at
        high = (at.high + at.highs - u) % at.highs

        def pick(t):
            low = (at.low + at.lows - t) % at.lows
            self.arrived(at.chunk(at.y, high, low))
            self.onward(at.y, high, low, False, True)

        each(at.lows, pick, 1)

    def from_y(self):
        at = self.at

        def one(t, v):
            y = (at.y + at.ys - t) % at.ys
            high = (at.high + at.highs - v % at.highs) % at.highs
            low = (at.low + v // at.highs) % at.lows
            self.arrived(at.chunk(y, high, low))
            self.onward(y, high, low, False, False)

        each(at.ys, lambda t: each(at.n_seq, lambda v: one(t, v)), 1)

    def from_core(self):
        at = self.at

        def one(t, v):
            core = (at.core + t) % at.cores
            self.arrived(((v // at.n_seq) * at.cores + core) * at.n_seq + v % at.n_seq)

        each(at.cores, lambda t: each(at.ys * at.n_seq, lambda v: one(t, v)), 1)

    def drain(self):
        at = self.at
        each(at.highs, lambda t: self.high_edge(t).wait_send(), 1)
        each(at.lows, lambda t: each(at.highs, lambda u: self.low_edge(t, u).wait_send()), 1)
        each(
            at.ys,
            lambda t: each(
                at.n_seq, lambda v: self.y_edge(t, v // at.lows, v % at.lows).wait_send()
            ),
            1,
        )
        each(
            at.cores,
            lambda t: each(
                at.ys * at.n_seq,
                lambda v: self.core_edge(t, v // at.n_seq, v % at.n_seq).wait_send(),
            ),
            1,
        )


class Scatter:
    def __init__(self, at, r):
        self.at, self.r = at, r

    def core_edge(self, t, y):
        at, r = self.at, self.r
        dp = y * at.cores + (at.core + t) % at.cores
        slot = t * at.ys + y
        return remote(
            r.grad.at[pl.ds(dp * at.n_seq, at.n_seq)], r.from_core.at[slot],
            r.gc_send.at[slot], r.gc_recv.at[slot], at.core_peer(t),
        )

    def y_edge(self, t, high, low):
        at, r = self.at, self.r
        slot = (t * at.highs + high) * at.lows + low
        return remote(
            r.staged1.at[slot], r.from1.at[slot],
            r.g1_send.at[slot], r.g1_recv.at[slot], at.y_peer(t),
        )

    def low_edge(self, t, high):
        at, r = self.at, self.r
        slot = t * at.highs + high
        return remote(
            r.staged2.at[slot], r.from2.at[slot],
            r.g2_send.at[slot], r.g2_recv.at[slot], at.low_peer(t),
        )

    def high_edge(self, t):
        at, r = self.at, self.r
        return remote(
            r.staged3.at[t], r.from3.at[t], r.g3_send.at[t], r.g3_recv.at[t], at.high_peer(t)
        )

    def chip_sum(self, y, high, low):
        at, r = self.at, self.r
        acc = r.grad[at.chunk(y, high, low)].astype(f32)
        for t in range(1, at.cores):
            acc = acc + r.from_core[t * at.ys + y, high * at.lows + low].astype(f32)
        return acc

    def y_sum(self, high, low):
        at, r = self.at, self.r
        acc = self.chip_sum(at.y, high, low)
        for t in range(1, at.ys):
            self.y_edge(t, high, low).wait_recv()
            acc = acc + r.from1[(t * at.highs + high) * at.lows + low].astype(f32)
        return acc

    def low_sum(self, high):
        at, r = self.at, self.r
        acc = self.y_sum(high, at.low)
        for t in range(1, at.lows):
            self.low_edge(t, high).wait_recv()
            acc = acc + r.from2[t * at.highs + high].astype(f32)
        return acc

    def to_y(self):
        at, r = self.at, self.r
        for t in range(1, at.cores):
            each(at.ys, lambda y: self.core_edge(t, y).wait_recv())

        def one(t, v):
            low = (at.low + 1 + v // at.highs) % at.lows
            high = (at.high + 1 + v) % at.highs
            acc = self.chip_sum((at.y + t) % at.ys, high, low)
            r.staged1[(t * at.highs + high) * at.lows + low] = acc.astype(bf16)
            self.y_edge(t, high, low).start()

        each(at.ys, lambda t: each(at.n_seq, lambda v: one(t, v)), 1)

    def to_low(self, u):
        at, r = self.at, self.r
        high = (at.high + 1 + u) % at.highs

        def one(t):
            low = (at.low + t) % at.lows
            r.staged2[t * at.highs + high] = self.y_sum(high, low).astype(bf16)
            self.low_edge(t, high).start()

        each(at.lows, one, 1)

    def to_high(self, t):
        at, r = self.at, self.r
        r.staged3[t] = self.low_sum((at.high + t) % at.highs).astype(bf16)
        self.high_edge(t).start()

    def finish(self):
        at, r = self.at, self.r
        acc = self.low_sum(at.high)
        each(at.highs, lambda t: self.high_edge(t).wait_recv(), 1)
        for t in range(1, at.highs):
            acc = acc + r.from3[t].astype(f32)
        r.acc[...] = acc
        return lane_total(total(fold(acc * acc)))

    def drain(self):
        at = self.at
        for t in range(1, at.cores):
            each(at.ys, lambda y: self.core_edge(t, y).wait_send())
        each(
            at.ys,
            lambda t: each(
                at.n_seq, lambda v: self.y_edge(t, v // at.lows, v % at.lows).wait_send()
            ),
            1,
        )
        each(at.lows, lambda t: each(at.highs, lambda u: self.low_edge(t, u).wait_send()), 1)
        each(at.highs, lambda t: self.high_edge(t).wait_send(), 1)


class Exchange:
    def __init__(self, at, reverse, state, landed, ready, entering, middle, sems):
        self.at, self.reverse = at, reverse
        self.state, self.landed, self.ready, self.entering = state, landed, ready, entering
        self.middle = middle
        self.s_send, self.s_recv, self.r_send, self.r_recv, self.m_send, self.m_recv = sems
        self.leader = 1 if reverse else 0

    def back(self, t):
        return (self.at.spot + self.at.group - t) % self.at.group

    def first(self, t):
        p = (self.at.spot + t) % self.at.group
        return remote(
            self.state.at[p], self.landed.at[self.at.spot],
            self.s_send.at[t], self.s_recv.at[t], self.at.group_peer(t),
        )

    def first_in(self, t):
        p = self.back(t)
        return remote(
            self.state.at[p], self.landed.at[p],
            self.s_send.at[t], self.s_recv.at[t], self.at.group_peer(t),
        )

    def second(self, t):
        p = (self.at.spot + t) % self.at.group
        return remote(
            self.ready.at[p], self.entering.at[self.at.spot],
            self.r_send.at[t], self.r_recv.at[t], self.at.group_peer(t),
        )

    def second_in(self, t):
        p = self.back(t)
        return remote(
            self.ready.at[p], self.entering.at[p],
            self.r_send.at[t], self.r_recv.at[t], self.at.group_peer(t),
        )

    def across(self):
        return remote(
            self.middle.at[0], self.middle.at[1],
            self.m_send.at[0], self.m_recv.at[0], self.at.other_half(),
        )

    def start(self):
        at = self.at
        each(at.group, lambda t: self.first(t).start(), 1)
        self.landed[at.spot] = self.state[at.spot]

    def lead(self, carries, size):
        @pl.when(self.at.part == self.leader)
        def _():
            self.turn(carries, size, True)

    def follow(self, carries, size):
        @pl.when(self.at.part != self.leader)
        def _():
            self.turn(carries, size, False)

    def turn(self, carries, size, leads):
        at = self.at
        mine, group = at.spot, at.group
        each(group, lambda t: self.first_in(t).wait_recv(), 1)
        if not leads:
            self.across().wait_recv()
        piece = self.state.shape[1]
        per = piece // size
        order = list(range(group))
        if self.reverse:
            order.reverse()
        for q in range(per):
            rows = slice(q * size, (q + 1) * size)
            if leads:
                running = jnp.zeros((size, self.state.shape[2]), f32)
            else:
                running = self.middle[1, rows, :].astype(f32)
            for n, d in enumerate(order):
                self.ready[d, rows, :] = running.astype(bf16)
                if leads or n < group - 1:
                    kept = carries[d, pl.ds(mine * per + q, 1), :]
                    running = kept * running + self.landed[d, rows, :].astype(f32)
            if leads:
                self.middle[0, rows, :] = running.astype(bf16)
        if leads:
            self.across().start()
        each(group, lambda t: self.second(t).start(), 1)
        self.entering[mine] = self.ready[mine]

    def finish(self):
        each(self.at.group, lambda t: self.second_in(t).wait_recv(), 1)

    def drain(self):
        each(self.at.group, lambda t: self.first(t).wait_send(), 1)
        each(self.at.group, lambda t: self.second(t).wait_send(), 1)

        @pl.when(self.at.part == self.leader)
        def _():
            self.across().wait_send()


def train_kernel(n_dp, n_seq, names, *refs):
    r = Refs(names, refs)
    at = Spot(n_dp, n_seq)
    inner, tokens = r.xt.shape
    heads = r.decay.shape[1]
    size = inner // heads
    ns = r.proj.shape[1] // 2
    share, model = r.rows.shape
    g = inner // LANES
    blocks = tokens // LANES
    head_rows = [slice(h * size, (h + 1) * size) for h in range(heads)]
    gather, scatter = Gather(at, r), Scatter(at, r)
    fore = Exchange(
        at, False, r.state, r.landed, r.ready, r.entering, r.middle,
        (r.s_send, r.s_recv, r.r_send, r.r_recv, r.m_send, r.m_recv),
    )
    rear = Exchange(
        at, True, r.b_state, r.b_landed, r.b_ready, r.leaving, r.b_middle,
        (r.bs_send, r.bs_recv, r.br_send, r.br_recv, r.bm_send, r.bm_recv),
    )
    b, c = slice(0, ns), slice(ns, 2 * ns)

    def wide(column):
        return jnp.concatenate([column] * blocks, axis=1)

    def lead(t):
        return remote(
            r.carries.at[at.spot], r.carries.at[at.spot],
            r.c_send.at[t], r.c_recv.at[t], at.group_peer(t),
        )

    def lead_in(t):
        p = (at.spot + at.group - t) % at.group
        return remote(
            r.carries.at[p], r.carries.at[p], r.c_send.at[t], r.c_recv.at[t], at.group_peer(t)
        )

    plane = n_dp * at.lows
    place = at.dp * at.lows + at.low

    def plane_edge(t, slot):
        return remote(
            r.gain_a.at[place], r.gain_a.at[slot],
            r.pa_send.at[t], r.pa_recv.at[t], at.plane_peer(t),
        )

    def line_edge(t, slot):
        return remote(
            r.gain_b.at[at.high], r.gain_b.at[slot],
            r.pb_send.at[t], r.pb_recv.at[t], at.high_peer(t),
        )

    def load(k, ref, to):
        return pltpu.make_async_copy(ref, to, r.l_sem.at[k])

    loads = [
        load(0, r.x_in, r.x), load(1, r.proj_in, r.proj),
        load(2, r.z_in, r.z), load(3, r.target_in, r.target),
    ]
    at.greet()
    for one in loads:
        one.start()
    r.held[...] = r.rows[...]
    for k, ref in enumerate((r.decay, r.bias, r.skip)):
        sub, lane = iota((heads, heads), 0), iota((heads, heads), 1)
        own = lane_total(jnp.where(sub == lane, ref[...], 0.0))
        row = to_row(own, k)
        packed = row if k == 0 else packed + row
    r.params[...] = packed
    r.gain_now[...] = r.gain[...]
    r.upper[...] = (iota((tokens, tokens), 0) <= iota((tokens, tokens), 1)).astype(bf16)
    loads[0].wait()
    for k in range(g):
        cols = slice(k * LANES, (k + 1) * LANES)
        r.xt[cols, :] = r.x[:, cols].astype(f32).T
    loads[1].wait()
    stop = jnp.where(r.ids[...] == 0, 1.0, 0.0)
    r.seg[...] = dot(jnp.broadcast_to(stop, (16, tokens)).astype(bf16), r.upper[...])

    def prepare():
        loads[2].wait()
        loads[3].wait()
        seg_c = r.seg[...].T[:, 0:1]
        raw = contract(r.proj[:, b], r.proj[:, c], 1, 1)
        open_to = (seg_c == r.seg[0:1, :]) & (
            iota((tokens, tokens), 0) <= iota((tokens, tokens), 1)
        )
        r.score[...] = jnp.where(open_to, raw, 0.0)
        for k in range(g):
            cols = slice(k * LANES, (k + 1) * LANES)
            zt = r.z[:, cols].astype(f32).T
            r.gate[cols, :] = zt * jax.nn.sigmoid(zt)

    def forward_head(h):
        rows = head_rows[h]
        for jb in range(blocks):
            js = slice(jb * LANES, (jb + 1) * LANES)
            left = r.sums_c[js, h : h + 1]
            for ib in range(jb, blocks):
                cs = slice(ib * LANES, (ib + 1) * LANES)
                gap = r.sums[h : h + 1, cs] - left
                if ib == jb:
                    gap = jnp.minimum(gap, 0.0)
                r.grid[h, js, cs] = (jnp.exp2(gap) * r.score[js, cs]).astype(bf16)
        for ib in range(blocks):
            end = (ib + 1) * LANES
            cs = slice(ib * LANES, end)
            r.mixed[rows, cs] = dot(r.scaled[rows, :end], r.grid[h, :end, cs])

    def backward_head(h):
        rows = head_rows[h]
        for jb in range(blocks):
            at_j = jb * LANES
            js = slice(at_j, at_j + LANES)
            part = contract(r.slope[rows, at_j:], r.grid[h, js, at_j:], 1, 1)
            r.col_dot[h : h + 1, js] = total(part * r.xt[rows, js])

    def own_state():
        packed = r.params[...]
        rate = -jnp.exp(jnp.broadcast_to(to_column(packed, 0, heads), (heads, tokens)))
        bias = jnp.broadcast_to(to_column(packed, 1, heads), (heads, tokens))
        w = jax.nn.softplus(r.raw_t[...] + bias)
        sums = accumulate(w * (rate * log2e), r.upper[...], 0)
        seg = r.seg[...][:heads]
        final = sums[:, tokens - 1 : tokens]
        last = seg[:, tokens - 1 : tokens]
        tail = jnp.where(seg == last, jnp.exp2(final - sums), 0.0)
        r.rate[...] = rate
        r.bias_w[...] = bias
        r.width[...] = w
        r.sums[...] = sums
        r.tail[...] = tail
        r.ending[...] = w * tail
        r.entry[...] = jnp.where(seg == 0.0, jnp.exp2(sums), 0.0)
        r.carries[at.spot] = jnp.broadcast_to(
            jnp.where(last == 0.0, jnp.exp2(final), 0.0), (heads, LANES)
        )
        for h in range(heads):
            rows = head_rows[h]
            r.slope[rows, :] = (r.xt[rows, :] * r.ending[h : h + 1, :]).astype(bf16)
        ended = dot(r.slope[...], r.proj[:, b])
        r.state[...] = ended.reshape(r.state.shape).astype(bf16)

    def open_step():
        each(at.group, lambda t: lead(t).start(), 1)
        fore.start()

    def step(s, _):
        r.sums_c[...] = r.sums[...].T
        for h in range(heads):
            rows = head_rows[h]
            r.scaled[rows, :] = (r.xt[rows, :] * r.width[h : h + 1, :]).astype(bf16)

        @pl.when(s == 0)
        def _():
            prepare()

        for k in range(g):
            row = jnp.broadcast_to(r.gain_now[k : k + 1, :], (LANES, LANES))
            r.gain_w[k * LANES : (k + 1) * LANES, :] = row.T
        cut = heads // 8
        marks = [slice(k * cut, (k + 1) * cut) for k in range(8)]

        def forward(k):
            for h in range(heads)[marks[k]]:
                forward_head(h)

        def backward(k):
            for h in range(heads)[marks[k]]:
                backward_head(h)

        forward(0)
        gather.from_low(0)
        forward(1)
        gather.from_high()
        each(at.group, lambda t: lead_in(t).wait_recv(), 1)
        fore.lead(r.carries, size)
        for u in range(1, at.highs):
            gather.from_low(u)
        for k in range(2, 5):
            forward(k)
        fore.follow(r.carries, size)
        for k in range(5, 8):
            forward(k)
        gather.from_y()
        fore.finish()

        passed = contract(flat(r.entering[...]), r.proj[:, c], 1, 1)
        skip = jnp.broadcast_to(to_column(r.params[...], 2, heads), (heads, tokens))
        r.skip_w[...] = skip
        power = jnp.zeros((8, tokens), f32)
        for h in range(heads):
            rows = head_rows[h]
            y = r.mixed[rows, :] + passed[rows, :] * r.entry[h : h + 1, :]
            r.mixed[rows, :] = y
            gated = (y + r.skip_w[h : h + 1, :] * r.xt[rows, :]) * r.gate[rows, :]
            r.gated[rows, :] = gated
            power = power + fold(gated * gated)
        root = lax.rsqrt(total(power) * (1.0 / inner) + norm_floor)
        r.root[...] = jnp.broadcast_to(root, r.root.shape)
        for k in range(g):
            rows = slice(k * LANES, (k + 1) * LANES)
            normed = r.gated[rows, :] * wide(r.gain_w[rows, :]) * r.root[0:1, :]
            r.normed[rows, :] = normed.astype(bf16)
            r.normed_n[:, rows] = normed.T.astype(bf16)

        gather.from_core()
        r.residual[...] = dot(r.normed_n[...], flat(r.full[...]))
        count = r.counts[0]
        for k in range(1, n_dp):
            count = count + r.counts[k]
        share_of = 1.0 / (model * count.astype(f32))
        limit = r.counts[at.dp] - at.seq * tokens
        lost = jnp.zeros((8, model), f32)
        step_rows = 32
        for q in range(tokens // step_rows):
            rows = slice(q * step_rows, (q + 1) * step_rows)
            scored = iota((step_rows, model), 0) + q * step_rows < limit
            gap = jnp.where(scored, r.residual[rows, :] - r.target[rows, :].astype(f32), 0.0)
            lost = lost + fold(gap * gap)
            r.og[rows, :] = (gap * (2.0 * share_of)).astype(bf16)
        loss = lane_total(total(lost)) * share_of

        def weight_part(t, y):
            dp = y * at.cores + (at.core + t) % at.cores
            width = n_seq * share
            left = r.normed[pl.ds(pl.multiple_of(dp * width, width), width), :]
            out = dot(left, r.og[...])
            r.grad[pl.ds(dp * n_seq, n_seq)] = out.reshape(n_seq, share, model).astype(bf16)
            if t > 0:
                scatter.core_edge(t, y).start()

        for t in range(1, at.cores):
            for u in range(at.ys):
                weight_part(t, (at.y + 1 + u) % at.ys)
        for u in range(at.ys):
            weight_part(0, (at.y + 1 + u) % at.ys)
        r.ng[...] = contract(flat(r.full[...]), r.og[...], 1, 1)
        scatter.to_y()
        inward = jnp.zeros((8, tokens), f32)
        for h in range(heads):
            rows = head_rows[h]
            lifted = r.ng[rows, :] * r.gated[rows, :]
            inward = inward + fold(lifted * wide(r.gain_w[rows, :]))
            lifted = lifted * r.root[0:1, :]
            part = lifted[:, :LANES]
            for k in range(1, blocks):
                part = part + lifted[:, k * LANES : (k + 1) * LANES]
            r.gain_part[rows, :] = part
        root = r.root[0:1, :]
        inward = total(inward) * (root * root * root * (1.0 / inner))
        r.inward[...] = jnp.broadcast_to(inward, r.inward.shape)
        for h in range(heads):
            rows = head_rows[h]
            dy = r.ng[rows, :] * wide(r.gain_w[rows, :]) * r.root[0:1, :]
            dy = (dy - r.gated[rows, :] * r.inward[0:1, :]) * r.gate[rows, :]
            r.row_dot[h : h + 1, :] = total(dy * r.mixed[rows, :])
            r.skip_dot[h : h + 1, :] = total(dy * r.xt[rows, :])
            r.slope[rows, :] = dy.astype(bf16)
            r.scaled[rows, :] = (dy * r.entry[h : h + 1, :]).astype(bf16)
        pulled = dot(r.scaled[...], r.proj[:, c])
        r.b_state[...] = pulled.reshape(r.b_state.shape).astype(bf16)
        rear.start()
        for k in range(g):
            rows = slice(k * LANES, (k + 1) * LANES)
            r.gain_a[place, k : k + 1, :] = total(r.gain_part[rows, :].T)
        each(plane, lambda t: plane_edge(t, place).start(), 1)
        backward(0)
        for u in range(at.highs):
            scatter.to_low(u)
            if u < 3:
                backward(u + 1)
            if u == 2:
                rear.lead(r.carries, size)
        backward(4)
        for t in range(1, at.highs):
            scatter.to_high(t)
        rear.follow(r.carries, size)
        for k in range(5, 8):
            backward(k)
        each(plane, lambda t: plane_edge(t, (place + plane - t) % plane).wait_recv(), 1)
        gain_sum = r.gain_a[0]
        for k in range(1, plane):
            gain_sum = gain_sum + r.gain_a[k]
        r.gain_b[at.high] = gain_sum
        each(at.highs, lambda t: line_edge(t, at.high).start(), 1)
        gather.drain()
        square = scatter.finish()
        rear.finish()

        after = flat(r.leaving[...])
        moved = contract(after, r.proj[:, b], 1, 1)
        for h in range(heads):
            rows = head_rows[h]
            r.pulled[h : h + 1, :] = total(moved[rows, :] * r.xt[rows, :])
        piece = r.leaving.shape[1]
        for h in range(heads):
            p, q = (h * size) // piece, (h * size) % piece
            own = r.leaving[p, q : q + size, :].astype(f32)
            own = own * r.entering[p, q : q + size, :].astype(f32)
            r.kept[h : h + 1, :] = total(own)
        drawn = r.pulled[...] * r.tail[...]
        w, rate = r.width[...], r.rate[...]
        col = r.col_dot[...] + drawn
        d_final = lane_total(w * drawn) + lane_total(r.kept[...] * r.carries[at.spot])
        d_rate = accumulate(r.row_dot[...] - w * col, r.upper[...], 1) + d_final
        d_width = (col + rate * d_rate) * jax.nn.sigmoid(r.raw_t[...] + r.bias_w[...])
        message = (
            to_row(lane_total(rate * d_rate * w), 0)
            + to_row(lane_total(d_width), 1)
            + to_row(lane_total(r.skip_dot[...]), 2)
        )
        lane = iota((1, LANES), 1)
        message = message + jnp.where(lane == 3 * heads, loss, 0.0)
        message = message + jnp.where(lane == 3 * heads + 1, square, 0.0)
        r.inbox[s, at.me] = message

        def news(t, slot):
            return remote(
                r.inbox.at[s, at.me], r.inbox.at[s, slot],
                r.n_send.at[t], r.n_recv.at[t], at.any_peer(t),
            )

        each(at.n, lambda t: news(t, at.me).start(), 1)
        each(at.highs, lambda t: line_edge(t, (at.high + at.highs - t) % at.highs).wait_recv(), 1)
        gain_sum = r.gain_b[0]
        for k in range(1, at.highs):
            gain_sum = gain_sum + r.gain_b[k]
        scatter.drain()
        fore.drain()
        rear.drain()
        each(at.group, lambda t: lead(t).wait_send(), 1)
        each(plane, lambda t: plane_edge(t, place).wait_send(), 1)
        each(at.highs, lambda t: line_edge(t, at.high).wait_send(), 1)
        each(at.n, lambda t: news(t, (at.me + at.n - t) % at.n).wait_recv(), 1)
        each(at.n, lambda t: news(t, at.me).wait_send(), 1)
        sums = jnp.sum(r.inbox[s], axis=0)
        small = jnp.where(lane < 3 * heads, sums, 0.0)
        norm = lane_total(small * small + total(gain_sum * gain_sum))
        norm = norm + lane_total(jnp.where(lane == 3 * heads + 1, sums, 0.0))
        pace = learn_rate * clip_limit / jnp.maximum(jnp.sqrt(norm), clip_limit)
        r.held[...] = r.held[...] - pace * r.acc[...]
        r.params[...] = r.params[...] - pace * small
        r.gain_now[...] = r.gain_now[...] - pace * gain_sum
        r.out_small[pl.ds(s + 1, 1), :] = jnp.broadcast_to(
            lane_total(jnp.where(lane == 3 * heads, sums, 0.0)), (1, LANES)
        )

        @pl.when(s < STEPS - 1)
        def _():
            r.full[at.me] = r.held[...].astype(bf16)
            gather.start()
            own_state()
            open_step()

        return 0

    r.full[at.me] = r.held[...].astype(bf16)
    own_state()
    at.meet()
    gather.start()
    open_step()
    lax.fori_loop(0, STEPS, step, 0)
    r.out_small[0:1, :] = r.params[...]
    r.out_gain[...] = r.gain_now[...]
    r.out_rows[...] = r.held[...]


def finish_kernel(rows, small, gain, losses, new_rows, decay, bias, skip, new_gain):
    heads = decay.shape[1]
    new_rows[...] = rows[...]
    new_gain[...] = gain[...]
    for k, ref in enumerate((decay, bias, skip)):
        ref[...] = small[0:1, k * heads : (k + 1) * heads]
    lane = iota((1, LANES), 1)
    both = jnp.where(lane == 0, small[1:2, :], small[2:3, :])
    losses[...] = both[:, :STEPS]


def call(body, outs, args, scratch=(), far=(), **extra):
    def place(k, a):
        if k in far:
            return pl.BlockSpec(memory_space=pl.ANY)
        return SMEM if a.ndim == 1 else VMEM

    return pl.pallas_call(
        body,
        out_shape=tuple(jax.ShapeDtypeStruct(*o) for o in outs),
        in_specs=[place(k, a) for k, a in enumerate(args)],
        out_specs=tuple([VMEM] * len(outs)),
        scratch_shapes=list(scratch),
        compiler_params=pltpu.CompilerParams(vmem_limit_bytes=LIMIT, **extra),
    )(*args)


def per_device(
    n_dp,
    n_seq,
    head_inputs,
    gate_inputs,
    state_proj,
    time_steps,
    token_ids,
    token_counts,
    teacher_out,
    out_weight,
    decay_log,
    step_bias,
    skip_gain,
    norm_gain,
):
    n = n_dp * n_seq
    x, z, target, raw = head_inputs[0], gate_inputs[0], teacher_out[0], time_steps[0]
    tokens, inner = x.shape
    ns = state_proj.shape[2] // 2
    heads = decay_log.shape[0]
    model = target.shape[1]
    share = out_weight.shape[0]
    group = n_seq // 2
    piece = inner // group
    g = inner // LANES
    cores = 2 if n_dp % 2 == 0 else 1
    ys = n_dp // cores
    highs = 4 if n_seq % 4 == 0 else n_seq
    lows = n_seq // highs
    per_head, tall = ((heads, tokens), f32), (inner, tokens)
    state = ((group, piece, ns), bf16)
    dma = pltpu.SemaphoreType.DMA
    vmem = {
        "x": (x.shape, bf16),
        "z": (z.shape, bf16),
        "target": (target.shape, bf16),
        "proj": (state_proj.shape[1:], bf16),
        "xt": (tall, f32),
        "gate": (tall, f32),
        "mixed": (tall, f32),
        "gated": (tall, f32),
        "ng": (tall, f32),
        "scaled": (tall, bf16),
        "slope": (tall, bf16),
        "normed": (tall, bf16),
        "normed_n": ((tokens, inner), bf16),
        "residual": ((tokens, model), f32),
        "og": ((tokens, model), bf16),
        "upper": ((tokens, tokens), bf16),
        "score": ((tokens, tokens), f32),
        "grid": ((heads, tokens, tokens), bf16),
        "seg": ((16, tokens), f32),
        "sums_c": ((tokens, heads), f32),
        "rate": per_head,
        "bias_w": per_head,
        "skip_w": per_head,
        "width": per_head,
        "sums": per_head,
        "tail": per_head,
        "ending": per_head,
        "entry": per_head,
        "row_dot": per_head,
        "skip_dot": per_head,
        "col_dot": per_head,
        "pulled": per_head,
        "kept": ((heads, ns), f32),
        "root": ((8, tokens), f32),
        "inward": ((8, tokens), f32),
        "gain_w": ((inner, LANES), f32),
        "gain_part": ((inner, LANES), f32),
        "gain_now": ((g, LANES), f32),
        "params": ((1, LANES), f32),
        "held": ((share, model), f32),
        "acc": ((share, model), f32),
        "full": ((n, share, model), bf16),
        "grad": ((n, share, model), bf16),
        "from_core": ((cores * ys, n_seq, share, model), bf16),
        "staged1": ((n // cores, share, model), bf16),
        "from1": ((n // cores, share, model), bf16),
        "staged2": ((n_seq, share, model), bf16),
        "from2": ((n_seq, share, model), bf16),
        "staged3": ((highs, share, model), bf16),
        "from3": ((highs, share, model), bf16),
        "middle": ((2, piece, ns), bf16),
        "b_middle": ((2, piece, ns), bf16),
        "state": state,
        "landed": state,
        "ready": state,
        "entering": state,
        "b_state": state,
        "b_landed": state,
        "b_ready": state,
        "leaving": state,
        "carries": ((group, heads, LANES), f32),
        "gain_a": ((n_dp * lows, g, LANES), f32),
        "gain_b": ((highs, g, LANES), f32),
        "inbox": ((STEPS, n, 1, LANES), f32),
    }
    sems = {
        "l_sem": (4,),
        "w_recv": (n,),
        "wz_send": (highs,),
        "wx_send": (n_seq,),
        "wy_send": (n // cores,),
        "wc_send": (n,),
        "gc_send": (cores * ys,),
        "gc_recv": (cores * ys,),
        "g1_send": (n // cores,),
        "g1_recv": (n // cores,),
        "g2_send": (n_seq,),
        "g2_recv": (n_seq,),
        "g3_send": (highs,),
        "g3_recv": (highs,),
        "m_send": (1,),
        "m_recv": (1,),
        "bm_send": (1,),
        "bm_recv": (1,),
        "pa_send": (n_dp * lows,),
        "pa_recv": (n_dp * lows,),
        "pb_send": (highs,),
        "pb_recv": (highs,),
        "n_send": (n,),
        "n_recv": (n,),
    }
    for name in ("c", "s", "r", "bs", "br"):
        sems[name + "_send"] = (group,)
        sems[name + "_recv"] = (group,)
    given = {
        "counts": token_counts,
        "decay": decay_log.reshape(1, heads),
        "bias": step_bias.reshape(1, heads),
        "skip": skip_gain.reshape(1, heads),
        "gain": norm_gain.reshape(g, LANES),
        "raw_t": raw.T,
        "ids": token_ids,
        "x_in": x,
        "z_in": z,
        "target_in": target,
        "proj_in": state_proj[0],
        "rows": out_weight,
    }
    outs = {
        "out_rows": ((share, model), f32),
        "out_small": ((8, LANES), f32),
        "out_gain": ((g, LANES), f32),
    }
    far = [k for k, name in enumerate(given) if name.endswith("_in")]
    names = [*given, *outs, *vmem, *sems]
    rows, small, gain = call(
        functools.partial(train_kernel, n_dp, n_seq, names),
        outs.values(),
        tuple(given.values()),
        [pltpu.VMEM(*v) for v in vmem.values()] + [dma(v) for v in sems.values()],
        far,
        collective_id=0,
        has_side_effects=True,
    )
    losses, rows, decay, bias, skip, gain = call(
        finish_kernel,
        [
            ((1, STEPS), f32),
            ((share, model), f32),
            ((1, heads), f32),
            ((1, heads), f32),
            ((1, heads), f32),
            ((g, LANES), f32),
        ],
        (rows, small, gain),
    )
    return (
        losses.reshape(STEPS),
        rows,
        decay.reshape(heads),
        bias.reshape(heads),
        skip.reshape(heads),
        gain.reshape(inner),
    )


def solution(mesh):
    in_specs = (
        P("dp", "seq", None),
        P("dp", "seq", None),
        P("dp", "seq", None),
        P("dp", "seq", None),
        P("dp", "seq"),
        P(),
        P("dp", "seq", None),
        P(("dp", "seq"), None),
        P(),
        P(),
        P(),
        P(),
    )
    out_specs = (P(), P(("dp", "seq"), None), P(), P(), P(), P())
    return jax.shard_map(
        functools.partial(per_device, mesh.shape["dp"], mesh.shape["seq"]),
        mesh=mesh,
        in_specs=in_specs,
        out_specs=out_specs,
        check_vma=False,
    )
```

time: 123 us -> 108 us (0.88)
  Pallas kernels: 122 us -> 108 us
    pallas_call x2, Pallas kernels: 122 us -> 108 us  [call(): pl.pallas_call(body, out_shape=tuple((jax.ShapeDtypeStruct(*o) for o in o...]
where the time goes in v2:
time: 108 us
  Pallas kernels  108 us (100%)
    pallas_call x2, Pallas kernels, call(): pl.pallas_call(body, out_shape=tuple((jax.ShapeDtypeStruct(*o) for o in o...  108 us

profile of v2, /device:TPU:0, one launch (start us, length us, event | category | flops | bytes accessed | tf_op | source)
XLA Modules:
  0.0 108.2 jit_solution(5782574349162457884)
XLA Ops:
  0.6 106.0 %shard_map.163 = (f32[32,1024]{1,0:T(8,128)}, f32[8,128]{1,0:T(8,128)}, f32[8,128]{1,0:T(8,128)}) custom-call(s32[4]{0:T(128)} %refs_0_.1, f32[1,16]{1,0:T(1,128)} %bitcast.22, f32[1,16]{1,0:T(1,128)} %bitcast.23, f32[1,16]{1,0:T(1,128)} %bitcast.24, f32[8,128]{1,0:T(8,128)} %bitcast.21, f32[16,384]{1,0:T(8,128)} %bitcast.20, s32[1,384]{1,0:T(1,128)} %refs_6_.1, ...), custom_call_target="tpu_custom_call" | custom-call | tf_op jit(solution)/shard_map/pallas_call | solution.py:866
  106.7 1.6 %shard_map.164 = (f32[1,2]{1,0:T(1,128)}, f32[32,1024]{1,0:T(8,128)}, f32[1,16]{1,0:T(1,128)}, f32[1,16]{1,0:T(1,128)}, f32[1,16]{1,0:T(1,128)}, /*index=5*/f32[8,128]{1,0:T(8,128)}) custom-call(f32[32,1024]{1,0:T(8,128)} %get-tuple-element.15.rows, f32[8,128]{1,0:T(8,128)} %get-tuple-element.16.small, f32[8,128]{1,0:T(8,128)} %get-tuple-element.17.gain), custom_call_target="tpu_custom_call" | custom-call | tf_op jit(solution)/shard_map/pallas_call | solution.py:866

commit v3 on v2

--- a/solution.py
+++ b/solution.py
@@ -125,18 +125,28 @@
     def chunk(self, y, high, low):
         return (y * self.cores + self.core) * self.n_seq + high * self.lows + low
 
+    def near(self):
+        return [
+            (self.highs, self.high_peer),
+            (self.group, self.group_peer),
+            (2, lambda t: self.other_half()),
+            (self.n_dp * self.lows, self.plane_peer),
+        ]
+
     def greet(self):
         barrier = pltpu.get_barrier_semaphore()
-        each(
-            self.n,
-            lambda t: pl.semaphore_signal(
-                barrier, inc=1, device_id=self.any_peer(t), device_id_type=MESH
-            ),
-            1,
-        )
+        for count, peer in self.near():
+            each(
+                count,
+                lambda t, peer=peer: pl.semaphore_signal(
+                    barrier, inc=1, device_id=peer(t), device_id_type=MESH
+                ),
+                1,
+            )
 
     def meet(self):
-        pl.semaphore_wait(pltpu.get_barrier_semaphore(), self.n - 1)
+        count = sum(count - 1 for count, _ in self.near())
+        pl.semaphore_wait(pltpu.get_barrier_semaphore(), count)
 
 
 def to_column(row, k, heads):
@@ -323,10 +333,13 @@
             acc = acc + r.from2[t * at.highs + high].astype(f32)
         return acc
 
+    def from_core(self, u):
+        at = self.at
+        each(at.cores, lambda t: self.core_edge(t, (at.y + u) % at.ys).wait_recv(), 1)
+
     def to_y(self):
         at, r = self.at, self.r
-        for t in range(1, at.cores):
-            each(at.ys, lambda y: self.core_edge(t, y).wait_recv())
+        each(at.ys, self.from_core, 1)
 
         def one(t, v):
             low = (at.low + 1 + v // at.highs) % at.lows
@@ -746,6 +759,7 @@
             r.gain_a[place, k : k + 1, :] = total(r.gain_part[rows, :].T)
         each(plane, lambda t: plane_edge(t, place).start(), 1)
         backward(0)
+        scatter.from_core(0)
         for u in range(at.highs):
             scatter.to_low(u)
             if u < 3:
@@ -816,15 +830,12 @@
         each(at.n, lambda t: news(t, at.me).wait_send(), 1)
         sums = jnp.sum(r.inbox[s], axis=0)
         small = jnp.where(lane < 3 * heads, sums, 0.0)
-        norm = lane_total(small * small + total(gain_sum * gain_sum))
-        norm = norm + lane_total(jnp.where(lane == 3 * heads + 1, sums, 0.0))
+        power = jnp.where(lane == 3 * heads + 1, sums, small * small)
+        norm = lane_total(power + total(gain_sum * gain_sum))
         pace = learn_rate * clip_limit / jnp.maximum(jnp.sqrt(norm), clip_limit)
         r.held[...] = r.held[...] - pace * r.acc[...]
         r.params[...] = r.params[...] - pace * small
         r.gain_now[...] = r.gain_now[...] - pace * gain_sum
-        r.out_small[pl.ds(s + 1, 1), :] = jnp.broadcast_to(
-            lane_total(jnp.where(lane == 3 * heads, sums, 0.0)), (1, LANES)
-        )
 
         @pl.when(s < STEPS - 1)
         def _():
@@ -833,6 +844,9 @@
             own_state()
             open_step()
 
+        r.out_small[pl.ds(s + 1, 1), :] = jnp.broadcast_to(
+            lane_total(jnp.where(lane == 3 * heads, sums, 0.0)), (1, LANES)
+        )
         return 0
 
     r.full[at.me] = r.held[...].astype(bf16)

time: 108 us -> 105 us (0.972)
  Pallas kernels: 108 us -> 104 us
    pallas_call x2, Pallas kernels: 108 us -> 104 us  [call(): pl.pallas_call(body, out_shape=tuple((jax.ShapeDtypeStruct(*o) for o in o...]
where the time goes in v3:
time: 105 us
  Pallas kernels  104 us (99%)
    pallas_call x2, Pallas kernels, call(): pl.pallas_call(body, out_shape=tuple((jax.ShapeDtypeStruct(*o) for o in o...  104 us

profile of v3, /device:TPU:0, one launch (start us, length us, event | category | flops | bytes accessed | tf_op | source)
XLA Modules:
  0.0 104.8 jit_solution(14960537595770724616)
XLA Ops:
  0.6 102.6 %shard_map.163 = (f32[32,1024]{1,0:T(8,128)}, f32[8,128]{1,0:T(8,128)}, f32[8,128]{1,0:T(8,128)}) custom-call(s32[4]{0:T(128)} %refs_0_.1, f32[1,16]{1,0:T(1,128)} %bitcast.22, f32[1,16]{1,0:T(1,128)} %bitcast.23, f32[1,16]{1,0:T(1,128)} %bitcast.24, f32[8,128]{1,0:T(8,128)} %bitcast.21, f32[16,384]{1,0:T(8,128)} %bitcast.20, s32[1,384]{1,0:T(1,128)} %refs_6_.1, ...), custom_call_target="tpu_custom_call" | custom-call | tf_op jit(solution)/shard_map/pallas_call | solution.py:880
  103.2 1.6 %shard_map.164 = (f32[1,2]{1,0:T(1,128)}, f32[32,1024]{1,0:T(8,128)}, f32[1,16]{1,0:T(1,128)}, f32[1,16]{1,0:T(1,128)}, f32[1,16]{1,0:T(1,128)}, /*index=5*/f32[8,128]{1,0:T(8,128)}) custom-call(f32[32,1024]{1,0:T(8,128)} %get-tuple-element.15.rows, f32[8,128]{1,0:T(8,128)} %get-tuple-element.16.small, f32[8,128]{1,0:T(8,128)} %get-tuple-element.17.gain), custom_call_target="tpu_custom_call" | custom-call | tf_op jit(solution)/shard_map/pallas_call | solution.py:880

commit v4 on v3

--- a/solution.py
+++ b/solution.py
@@ -754,10 +754,6 @@
         pulled = dot(r.scaled[...], r.proj[:, c])
         r.b_state[...] = pulled.reshape(r.b_state.shape).astype(bf16)
         rear.start()
-        for k in range(g):
-            rows = slice(k * LANES, (k + 1) * LANES)
-            r.gain_a[place, k : k + 1, :] = total(r.gain_part[rows, :].T)
-        each(plane, lambda t: plane_edge(t, place).start(), 1)
         backward(0)
         scatter.from_core(0)
         for u in range(at.highs):
@@ -767,6 +763,10 @@
             if u == 2:
                 rear.lead(r.carries, size)
         backward(4)
+        for k in range(g):
+            rows = slice(k * LANES, (k + 1) * LANES)
+            r.gain_a[place, k : k + 1, :] = total(r.gain_part[rows, :].T)
+        each(plane, lambda t: plane_edge(t, place).start(), 1)
         for t in range(1, at.highs):
             scatter.to_high(t)
         rear.follow(r.carries, size)

time: 105 us -> 105 us (level)
  no operation moved by 1% of the time
where the time goes in v4:
time: 105 us; the launch traced here: 104 us
  Pallas kernels  104 us (99%)
    pallas_call x2, Pallas kernels, call(): pl.pallas_call(body, out_shape=tuple((jax.ShapeDtypeStruct(*o) for o in o...  104 us

profile of v4, /device:TPU:0, one launch (start us, length us, event | category | flops | bytes accessed | tf_op | source)
XLA Modules:
  0.0 104.4 jit_solution(11622337135064751993)
XLA Ops:
  0.6 102.2 %shard_map.163 = (f32[32,1024]{1,0:T(8,128)}, f32[8,128]{1,0:T(8,128)}, f32[8,128]{1,0:T(8,128)}) custom-call(s32[4]{0:T(128)} %refs_0_.1, f32[1,16]{1,0:T(1,128)} %bitcast.22, f32[1,16]{1,0:T(1,128)} %bitcast.23, f32[1,16]{1,0:T(1,128)} %bitcast.24, f32[8,128]{1,0:T(8,128)} %bitcast.21, f32[16,384]{1,0:T(8,128)} %bitcast.20, s32[1,384]{1,0:T(1,128)} %refs_6_.1, ...), custom_call_target="tpu_custom_call" | custom-call | tf_op jit(solution)/shard_map/pallas_call | solution.py:880
  102.9 1.6 %shard_map.164 = (f32[1,2]{1,0:T(1,128)}, f32[32,1024]{1,0:T(8,128)}, f32[1,16]{1,0:T(1,128)}, f32[1,16]{1,0:T(1,128)}, f32[1,16]{1,0:T(1,128)}, /*index=5*/f32[8,128]{1,0:T(8,128)}) custom-call(f32[32,1024]{1,0:T(8,128)} %get-tuple-element.15.rows, f32[8,128]{1,0:T(8,128)} %get-tuple-element.16.small, f32[8,128]{1,0:T(8,128)} %get-tuple-element.17.gain), custom_call_target="tpu_custom_call" | custom-call | tf_op jit(solution)/shard_map/pallas_call | solution.py:880
